TPU v7x, 32 devices: a 4x4x1 block of a 4x4x8 slice. The times are simulated.
32 devices in a mesh: dp: 1 (over z), tph: 4 (over y), tpw: 8 (over x, core).
Axes of the slice: x: 4, y: 4, z: 1, core: 2. Of those that a mesh axis runs over, the one named last changes fastest.
The devices are a block of a 4x4x8 slice.
Arguments:
- x_in: bfloat16 [128, 8192], P('dp', 'tpw')
- ln_attn: float32 [2, 8192], P(None, 'tpw')
- ln_mlp: float32 [2, 8192], P(None, 'tpw')
- w_qkv: bfloat16 [8192, 8, 18, 64], P('tpw', 'tph')
- w_out: bfloat16 [8, 16, 64, 8192], P('tph', None, None, 'tpw')
- w_up: bfloat16 [8192, 32768], P('tpw', 'tph')
- w_down: bfloat16 [32768, 8192], P('tph', 'tpw')
- k_cache: bfloat16 [128, 8, 512, 64], P(('dp', 'tpw'), 'tph')
- v_cache: bfloat16 [128, 8, 512, 64], P(('dp', 'tpw'), 'tph')
- positions: int32 [128], P(('dp', 'tpw'))
Outputs:
- output 1: bfloat16 [128, 8192], P('dp', 'tpw')
- output 2: bfloat16 [128, 8, 64], P(('dp', 'tpw'), 'tph')
- output 3: bfloat16 [128, 8, 64], P(('dp', 'tpw'), 'tph')
All inputs are finite; a program needn't handle non-finite values.
Results may differ from a plain program's by a relative error of at most 0.013997.
Values are sent between devices in bfloat16 or wider.
A program may use at most 768 MiB of HBM per device.

v0:
```python
import jax
import jax.numpy as jnp
from jax import lax
from jax.sharding import PartitionSpec as P

LN_EPS = 1e-5
ROPE_BASE = 10000.0


def normalize(x_f32, row_stats, model_width):
    row_mean = row_stats[:, 0:1] / model_width
    row_var = row_stats[:, 1:2] / model_width - row_mean * row_mean
    return (x_f32 - row_mean) * lax.rsqrt(row_var + LN_EPS)


def rope_tables(positions, head_dim):
    half_dim = head_dim // 2
    inv_freq = ROPE_BASE ** (-jnp.arange(half_dim, dtype=jnp.float32) * (2.0 / head_dim))
    angles = positions.astype(jnp.float32)[:, None] * inv_freq[None, :]
    return jnp.cos(angles), jnp.sin(angles)


def rotary(vectors, cos_t, sin_t):
    half_dim = vectors.shape[-1] // 2
    lo_half = vectors[..., :half_dim]
    hi_half = vectors[..., half_dim:]
    return jnp.concatenate([lo_half * cos_t - hi_half * sin_t, hi_half * cos_t + lo_half * sin_t], axis=-1)


def attend(qkv_rows, k_cache, v_cache, positions):
    q_count = qkv_rows.shape[2] - 2
    head_dim = qkv_rows.shape[3]
    cache_len = k_cache.shape[2]
    cos_t, sin_t = rope_tables(positions, head_dim)
    qkv_f32 = qkv_rows.astype(jnp.float32)
    q_rot = rotary(qkv_f32[:, :, :q_count], cos_t[:, None, None, :], sin_t[:, None, None, :]).astype(jnp.bfloat16)
    k_new = rotary(qkv_f32[:, :, q_count], cos_t[:, None, :], sin_t[:, None, :]).astype(jnp.bfloat16)
    v_new = qkv_rows[:, :, q_count + 1]
    attn_scale = head_dim ** -0.5
    old_scores = jnp.einsum("bgqh,bgsh->bgqs", q_rot, k_cache, preferred_element_type=jnp.float32) * attn_scale
    visible = jnp.arange(cache_len)[None, None, None, :] < positions[:, None, None, None]
    old_scores = jnp.where(visible, old_scores, -jnp.inf)
    new_score = jnp.einsum("bgqh,bgh->bgq", q_rot, k_new, preferred_element_type=jnp.float32) * attn_scale
    row_max = jnp.maximum(old_scores.max(axis=-1), new_score)
    e_old = jnp.exp(old_scores - row_max[..., None])
    e_new = jnp.exp(new_score - row_max)
    norm_sum = e_old.sum(axis=-1) + e_new
    w_old = (e_old / norm_sum[..., None]).astype(jnp.bfloat16)
    w_new = (e_new / norm_sum).astype(jnp.bfloat16)
    context = jnp.einsum("bgqs,bgsh->bgqh", w_old, v_cache, preferred_element_type=jnp.float32)
    context = context + w_new.astype(jnp.float32)[..., None] * v_new.astype(jnp.float32)[:, :, None, :]
    return context.astype(jnp.bfloat16), k_new, v_new


def solution(mesh):
    width_devices = mesh.shape["tpw"]

    def local_layer(x_in, ln_attn, ln_mlp, w_qkv, w_out, w_up, w_down, k_cache, v_cache, positions):
        model_width = x_in.shape[1] * width_devices
        x_f32 = x_in.astype(jnp.float32)
        row_stats = jnp.stack([x_f32.sum(axis=-1), (x_f32 * x_f32).sum(axis=-1)], axis=-1)
        row_stats = lax.psum(row_stats, "tpw")
        centered = normalize(x_f32, row_stats, model_width)
        h_attn = (centered * ln_attn[0] + ln_attn[1]).astype(jnp.bfloat16)
        h_mlp = (centered * ln_mlp[0] + ln_mlp[1]).astype(jnp.bfloat16)
        qkv_part = jnp.einsum("bd,dgjh->bgjh", h_attn, w_qkv, preferred_element_type=jnp.float32)
        qkv_rows = lax.psum_scatter(qkv_part.astype(jnp.bfloat16), "tpw", scatter_dimension=0, tiled=True)
        context, k_new, v_new = attend(qkv_rows, k_cache, v_cache, positions)
        context_all = lax.all_gather(context, "tpw", axis=0, tiled=True)
        attn_part = jnp.einsum("bgqh,gqhd->bd", context_all, w_out, preferred_element_type=jnp.float32)
        pre_part = jnp.dot(h_mlp, w_up, preferred_element_type=jnp.float32)
        pre_act = lax.psum(pre_part.astype(jnp.bfloat16), "tpw")
        act_bf = jax.nn.gelu(pre_act.astype(jnp.float32), approximate=False).astype(jnp.bfloat16)
        mlp_part = jnp.dot(act_bf, w_down, preferred_element_type=jnp.float32)
        branch = lax.psum((attn_part + mlp_part).astype(jnp.bfloat16), "tph")
        x_out = (x_f32 + branch.astype(jnp.float32)).astype(jnp.bfloat16)
        return x_out, k_new, v_new

    cache_spec = P(("dp", "tpw"), "tph", None, None)
    new_spec = P(("dp", "tpw"), "tph", None)
    in_specs = (
        P("dp", "tpw"),
        P(None, "tpw"),
        P(None, "tpw"),
        P("tpw", "tph", None, None),
        P("tph", None, None, "tpw"),
        P("tpw", "tph"),
        P("tph", "tpw"),
        cache_spec,
        cache_spec,
        P(("dp", "tpw")),
    )
    out_specs = (P("dp", "tpw"), new_spec, new_spec)
    return jax.shard_map(local_layer, mesh=mesh, in_specs=in_specs, out_specs=out_specs, check_vma=False)
```

profile of v0, /device:TPU:97, one launch (start us, length us, event | category | flops | bytes accessed | tf_op | source)
XLA Modules:
  0.0 183.4 jit_solution(17370132375769089877)
XLA Ops:
  7.3 1.2 convert_reduce_fusion
  8.5 13.9 %psum.21 = f32[128,2]{0,1:T(2,128)S(1)} all-reduce(f32[128,2]{0,1:T(2,128)S(1)} %pad_maximum_fusion.2), channel_id=1, replica_groups=mesh['dp'=1,'tph'=4,'tpw'=8] {'tpw'}, use_global_device_ids=true, to_apply=%region_2.0 | all-reduce | flops 256 | bytes 2048 | tf_op jit(solution)/shard_map/psum | solution.py:62
  22.4 0.8 fusion.134
  23.2 6.0 %convolution_convert_fusion.1 = bf16[128,2,18,64]{3,0,2,1:T(8,128)(2,1)} fusion(bf16[1024,2,18,64]{0,3,2,1:T(8,128)(2,1)} %param.13, bf16[128,1024]{1,0:T(8,128)(2,1)} %param.10, f32[1024]{0:T(1024)S(1)} %bitcast.41, f32[1024]{0:T(1024)S(1)} %bitcast.40, f32[128]{0:T(128)S(1)} %get-tuple-element.23, f32[128]{0:T(128)S(1)} %get-tuple-element.22), kind=kOutput, calls=%fused_computation.66 | convolution fusion | flops 605061120 | bytes 5579776 | tf_op jit(solution)/shard_map/bd,dgjh->bgjh/dot_general | solution.py:66
  29.4 9.5 %convolution_convert_fusion = bf16[128,8192]{1,0:T(8,128)(2,1)} fusion(bf16[1024,8192]{1,0:T(8,128)(2,1)} %param.15, bf16[128,1024]{1,0:T(8,128)(2,1)S(1)} %copy-done.1, f32[1024]{0:T(1024)S(1)} %bitcast.37, f32[1024]{0:T(1024)S(1)} %bitcast.36, f32[128]{0:T(128)S(1)} %get-tuple-element.23, f32[128]{0:T(128)S(1)} %get-tuple-element.22), kind=kOutput, calls=%fused_computation | convolution fusion | flops 2149318656 | bytes 19145728 | tf_op jit(solution)/shard_map/dot_general | solution.py:71
  39.1 0.1 multiply_cosine_fusion
  39.3 19.6 %reduce-scatter.2.cloned.1.call-done = bf16[16,2,18,64]{3,0,2,1:T(8,128)(2,1)} async-done(((bf16[128,2,18,64]{3,0,2,1:T(8,128)(2,1)}), bf16[16,2,18,64]{3,0,2,1:T(8,128)(2,1)}) %reduce-scatter.2.cloned.1.call-update) | async-done | bytes 73744 | tf_op jit(solution)/shard_map/reduce_scatter | solution.py:67
  58.9 1.1 convert_element_type.55
  59.9 0.1 subtract_convert_fusion
  60.2 0.1 pad_maximum_fusion
  60.4 0.2 fusion.95
  60.6 0.5 fusion.135
  61.1 0.4 fusion.70
  61.5 0.7 fusion.80
  62.3 0.7 slice_bitcast_fusion.1
  63.0 0.2 fusion.86
  63.2 22.8 %all_gather.3 = bf16[128,2,16,64]{3,0,2,1:T(8,128)(2,1)S(1)} all-gather(bf16[16,2,16,64]{3,0,2,1:T(8,128)(2,1)S(1)} %fusion.86), channel_id=1, replica_groups=mesh['dp'=1,'tph'=4,'tpw'=8] {'tpw'}, dimensions={0}, use_global_device_ids=true | all-gather | bytes 589824 | tf_op jit(solution)/shard_map/all_gather | solution.py:69
  86.1 3.0 %convolution_bitcast_fusion = f32[128,1024]{1,0:T(8,128)S(1)} fusion(bf16[128,2,16,64]{3,0,2,1:T(8,128)(2,1)S(1)} %all_gather.3, bf16[2,16,64,1024]{3,2,1,0:T(8,128)(2,1)} %param.14), kind=kOutput, calls=%fused_computation.69 | convolution fusion | flops 536870912 | bytes 5242880 | tf_op jit(solution)/shard_map/bgqh,gqhd->bd/dot_general | solution.py:70
  89.0 34.7 %all-reduce.3.cloned.1.call-done = bf16[128,8192]{1,0:T(8,128)(2,1)} async-done(((bf16[128,8192]{1,0:T(8,128)(2,1)}), bf16[128,8192]{1,0:T(8,128)(2,1)}) %all-reduce.3.cloned.1.call-update) | async-done | bytes 2097168 | tf_op jit(solution)/shard_map/psum | solution.py:72
  123.8 15.0 %fusion.67 = bf16[128,1024]{1,0:T(8,128)(2,1)} fusion(f32[128,1024]{1,0:T(8,128)S(1)} %convolution_bitcast_fusion, bf16[8192,1024]{1,0:T(8,128)(2,1)} %param.16, bf16[128,8192]{1,0:T(8,128)(2,1)} %all-reduce.3.cloned.1.call-done), kind=kOutput, calls=%fused_computation.71 | convolution fusion | flops 2216951808 | bytes 19660800 | tf_op jit(solution)/shard_map/dot_general | solution.py:74
  138.8 0.6 copy.16
  139.5 0.6 copy.15
  140.1 35.0 %all-reduce.5.cloned.1.call-done = bf16[128,1024]{1,0:T(8,128)(2,1)} async-done(((bf16[128,1024]{1,0:T(8,128)(2,1)}), bf16[128,1024]{1,0:T(8,128)(2,1)}) %all-reduce.5.cloned.1.call-update) | async-done | bytes 262160 | tf_op jit(solution)/shard_map/psum | solution.py:75
  175.1 1.7 fusion.79
  (29 shorter events, 0.9 us)
Async XLA Ops:
  7.2 53.4 %copy-start = (bf16[16,2,512,64]{2,3,1,0:T(8,128)(2,1)S(1)}, bf16[16,2,512,64]{2,3,1,0:T(8,128)(2,1)}, u32[]{:S(2)}) copy-start(bf16[16,2,512,64]{2,3,1,0:T(8,128)(2,1)} %param.17) | copy-start | bytes 6291460
  7.2 51.7 %reduce-scatter.2.cloned.1.call-start = ((), (), s32[]{:S(2)}) async-start(), calls=%async_computation.1 | async-start | bytes 1327104 | tf_op jit(solution)/shard_map/reduce_scatter | solution.py:67
  23.2 6.1 %copy-start.2 = (f32[2,1024]{1,0:T(2,128)S(1)}, f32[2,1024]{1,0:T(2,128)}, u32[]{:S(2)}) copy-start(f32[2,1024]{1,0:T(2,128)} %param.12) | copy-start | bytes 24580
  23.2 6.2 %copy-start.1 = (bf16[128,1024]{1,0:T(8,128)(2,1)S(1)}, bf16[128,1024]{1,0:T(8,128)(2,1)}, u32[]{:S(2)}) copy-start(bf16[128,1024]{1,0:T(8,128)(2,1)} %param.10) | copy-start | bytes 786436
  29.2 94.6 %all-reduce.3.cloned.1.call-start = ((), (), s32[]{:S(2)}) async-start(), calls=%async_computation.2 | async-start | bytes 4194304 | tf_op jit(solution)/shard_map/psum | solution.py:72
  29.3 9.7 %copy-start.3 = (s32[16]{0:T(128)S(1)}, s32[16]{0:T(128)}, u32[]{:S(2)}) copy-start(s32[16]{0:T(128)} %param.19) | copy-start | bytes 196
  39.0 136.2 %all-reduce.5.cloned.1.call-start = ((), (), s32[]{:S(2)}) async-start(), calls=%async_computation.3 | async-start | bytes 524288 | tf_op jit(solution)/shard_map/psum | solution.py:75
  58.8 2.7 %copy-start.4 = (bf16[16,2,512,64]{2,3,1,0:T(8,128)(2,1)S(1)}, bf16[16,2,512,64]{2,3,1,0:T(8,128)(2,1)}, u32[]{:S(2)}) copy-start(bf16[16,2,512,64]{2,3,1,0:T(8,128)(2,1)} %param.18) | copy-start | bytes 6291460
Sparse Core Ops, SparseCore 0:
  29.4 29.4 reduce-scatter.1
  61.2 62.4 all-reduce.2
  139.0 36.1 all-reduce.4
where the time goes:
time: 185 us; the launch traced here: 183 us
  waiting for transfers between devices  89.5 us (48%)
  blocking collectives  36.7 us (20%)
  matrix products  34.9 us (19%)
  between operations  13.9 us (8%)
  other arithmetic  6.08 us (3%)
  local copies, waits for them, and re-layouts  2.12 us (1%)
    psum x1, waiting for transfers between devices, local_layer(): branch = lax.psum((attn_part + mlp_part).astype(jnp.bfloat16), 'tph')  35 us
    psum x1, waiting for transfers between devices, local_layer(): pre_act = lax.psum(pre_part.astype(jnp.bfloat16), 'tpw')  34.7 us
    all_gather x1, blocking collectives, local_layer(): context_all = lax.all_gather(context, 'tpw', axis=0, tiled=True)  22.8 us
    reduce_scatter x1, waiting for transfers between devices, local_layer(): lax.psum_scatter(qkv_part.astype(jnp.bfloat16), 'tpw', scatter_dimension=...  19.6 us
    dot_general x1, matrix products, local_layer(): mlp_part = jnp.dot(act_bf, w_down, preferred_element_type=jnp.float32)  15 us
    psum x1, blocking collectives, local_layer(): row_stats = lax.psum(row_stats, 'tpw')  13.9 us
    dot_general x1, matrix products, local_layer(): pre_part = jnp.dot(h_mlp, w_up, preferred_element_type=jnp.float32)  9.54 us
    dot_general x1, matrix products, local_layer(): jnp.einsum('bd,dgjh->bgjh', h_attn, w_qkv, preferred_element_type=jnp.flo...  5.98 us
  transfers between devices with their start and end apart: 3, of which 3 were waited for; matrix products, arithmetic and copies ran while one was open for 10% of the time, Pallas kernels for 0%

commit v1 on v0

v1 whole, which is shorter than its diff:
```python
import functools
import math

import jax
import jax.numpy as jnp
from jax import lax
from jax.experimental import pallas as pl
from jax.experimental.pallas import tpu as pltpu
from jax.sharding import PartitionSpec as P

LN_EPS = 1e-5
ROPE_BASE = 10000.0
MESH = pl.DeviceIdType.MESH
F32 = jnp.float32
BF16 = jnp.bfloat16
VMEM_LIMIT = 67043328
GROUPS_OF_ROWS = 2
NN = (((1,), (0,)), ((), ()))
NT = (((1,), (1,)), ((), ()))
PIECES = ((2, 0), (2, 1), (1, 1), (3, 0), (1, 0), (3, 1), (0, 0), (0, 1))
ARRIVALS = ((0, 0), (0, 1), (3, 0), (1, 1), (3, 1), (1, 0), (2, 0), (2, 1))


def dot(a, b, dims=NN):
    return lax.dot_general(a, b, dims, preferred_element_type=F32)


def layer_kernel(
    W, NY,
    pos_ref, x_hbm, lna_hbm, lnm_hbm, wqkv_hbm, wout_hbm, wup_hbm, wdn_hbm, k_hbm, v_hbm,
    xout_ref, knew_ref, vnew_ref,
    x_v, lna_v, lnm_v, wqkv_v, wout_v, wup_v, wdn_v, k_v, v_v,
    stat_send, stat_recv, ha_v, hm_v,
    qpart, qsib, qsend, qrecv, qrot, kvrot, ctxs, ctx_all,
    upart, usib, usend, urecv, act_all, acc, ysend, yrecv,
    lsem, ssem, rsem,
):
    NX = W // 2
    R, D = x_v.shape
    NG = GROUPS_OF_ROWS
    RG = R // NG
    RY = RG // NY
    RB = R // W
    G, HD = kvrot.shape[0], k_v.shape[1]
    L = k_v.shape[2]
    QT = qrot.shape[1] // RB
    HB = wup_v.shape[2] // 2
    model_width = float(D * W)

    w = lax.axis_index("tpw")
    y = lax.axis_index("tph")
    c = lax.rem(w, 2)
    x = lax.div(w, 2)
    sib = w + 1 - 2 * c
    right = lax.rem(w + 2, W)
    left = lax.rem(w + W - 2, W)
    opp = lax.rem(w + W // 2, W)

    def chip(o):
        return lax.rem(x + o, NX)

    loads = {}

    def load(name, src, dst):
        cp = pltpu.make_async_copy(src, dst, lsem.at[len(loads)])
        cp.start()
        loads[name] = cp

    load("x", x_hbm, x_v)
    load("lna", lna_hbm, lna_v)
    load("lnm", lnm_hbm, lnm_v)
    qw = wqkv_v.shape[1]
    for g in range(G):
        load(("qkv", g), wqkv_hbm.at[pl.ds(g * qw, qw), :], wqkv_v.at[g])
    for i, (o, h) in enumerate(PIECES):
        col = pl.multiple_of((chip(o) * 2 + h) * 2 * HB, 2 * HB)
        load(("up", i), wup_hbm.at[:, pl.ds(col, 2 * HB)], wup_v.at[i])
    load("k", k_hbm, k_v)
    load("v", v_hbm, v_v)
    load("out", wout_hbm, wout_v)
    for i, (o, h) in enumerate(ARRIVALS):
        row = pl.multiple_of((chip(o) * 2 + h) * 2 * HB, 2 * HB)
        load(("down", i), wdn_hbm.at[pl.ds(row, 2 * HB), :], wdn_v.at[i])

    barrier = pltpu.get_barrier_semaphore()
    for i in range(1, W):
        pl.semaphore_signal(barrier, inc=1, device_id={"tpw": lax.rem(w + i, W)}, device_id_type=MESH)
    for i in range(1, NY):
        pl.semaphore_signal(barrier, inc=1, device_id={"tph": lax.rem(y + i, NY)}, device_id_type=MESH)

    sent = []
    messages = {}

    def send(name, src, dst, axis, to):
        i = len(sent)
        cp = pltpu.make_async_remote_copy(
            src_ref=src, dst_ref=dst, send_sem=ssem.at[i], recv_sem=rsem.at[i],
            device_id={axis: to}, device_id_type=MESH,
        )
        cp.start()
        sent.append(cp)
        messages[name] = cp

    def arrived(name):
        messages[name].wait_recv()

    loads["x"].wait()
    xf = x_v[...].astype(F32)
    s1 = jnp.sum(xf, axis=1, keepdims=True)
    s2 = jnp.sum(xf * xf, axis=1, keepdims=True)
    lane = lax.broadcasted_iota(jnp.int32, (R, 128), 1)
    stat_send[...] = jnp.where(lane == 0, s1, jnp.where(lane == 1, s2, 0.0)).T[0:8, :]
    pl.semaphore_wait(barrier, W - 1 + NY - 1)
    for i in range(1, W):
        send(("stat", i), stat_send, stat_recv.at[i - 1], "tpw", lax.rem(w + i, W))

    prow = lax.broadcasted_iota(jnp.int32, (RB, 128), 0)
    plane = lax.broadcasted_iota(jnp.int32, (RB, 128), 1)
    pos = jnp.zeros((RB, 128), jnp.int32)
    for b in range(RB):
        pos = jnp.where(prow == b, pos_ref[b], pos)
    half = HD // 2
    freq = jnp.exp(lax.rem(plane, half).astype(F32) * (-math.log(ROPE_BASE) * 2.0 / HD))
    angle = pos.astype(F32) * freq
    cos_t = jnp.cos(angle)
    first = lax.rem(plane, HD) < half
    sin_t = jnp.where(first, -jnp.sin(angle), jnp.sin(angle))

    for i in range(1, W):
        arrived(("stat", i))
    tot = stat_send[...]
    for i in range(1, W):
        tot = tot + stat_recv[i - 1]
    cols = jnp.concatenate([tot, jnp.zeros((R - 8, R), F32)], axis=0).T
    mean = cols[:, 0:1] / model_width
    var = cols[:, 1:2] / model_width - mean * mean
    rstd = lax.rsqrt(var + LN_EPS)
    loads["lna"].wait()
    loads["lnm"].wait()
    cen = (x_v[...].astype(F32) - mean) * rstd
    ha_v[...] = (cen * lna_v[0:1, :] + lna_v[1:2, :]).astype(BF16)
    hm_v[...] = (cen * lnm_v[0:1, :] + lnm_v[1:2, :]).astype(BF16)

    def tree(tag, own, stage, landing):
        def m1():
            stage[0] = own(2, 0).astype(BF16)
            send((tag, 0), stage.at[0], landing.at[0], "tpw", right)
            stage[1] = own(2, 1).astype(BF16)
            send((tag, 1), stage.at[1], landing.at[1], "tpw", left)

        def m2():
            stage[2] = own(1, 1).astype(BF16)
            send((tag, 2), stage.at[2], landing.at[2], "tpw", right)
            stage[3] = own(3, 0).astype(BF16)
            send((tag, 3), stage.at[3], landing.at[3], "tpw", left)

        def m3():
            arrived((tag, 0))
            stage[4] = (own(1, 0) + landing[0].astype(F32)).astype(BF16)
            send((tag, 4), stage.at[4], landing.at[4], "tpw", right)
            arrived((tag, 1))
            stage[5] = (own(3, 1) + landing[1].astype(F32)).astype(BF16)
            send((tag, 5), stage.at[5], landing.at[5], "tpw", left)

        def total(h):
            a, b = ((3, 4), (2, 5))[h]
            arrived((tag, a))
            arrived((tag, b))
            return own(0, h) + landing[a].astype(F32) + landing[b].astype(F32)

        return m1, m2, m3, total

    def qkv_mm(g):
        loads[("qkv", g)].wait()
        part = dot(ha_v[...], wqkv_v[g], NT).astype(BF16)
        qpart[g] = part.reshape(NX, 2, RB, qw)
        send(("qs", g), qpart.at[g, :, 1 - c], qsib.at[g], "tpw", sib)

    def qkv_own(o, g):
        return qpart[g, chip(o), c].astype(F32) + qsib[g, chip(o)].astype(F32)

    q1, q2, q3, q_total = tree("q", qkv_own, qsend, qrecv)

    def up_mm(r, i):
        if r == 0:
            loads[("up", i)].wait()
        hm = hm_v[r * RG:(r + 1) * RG, :]
        for k in range(2):
            upart[r, i, k] = dot(hm, wup_v[i, :, k * HB:(k + 1) * HB]).astype(BF16)
        send(("us", r, i), upart.at[r, i, 1 - c], usib.at[r, i], "tpw", sib)

    def up_tree(r):
        waited = set()

        def own(o, h):
            i = PIECES.index((o, h))
            if i not in waited:
                arrived(("us", r, i))
                waited.add(i)
            return upart[r, i, c].astype(F32) + usib[r, i].astype(F32)

        return tree(("u", r), own, usend.at[r], urecv.at[r])

    trees = [up_tree(r) for r in range(NG)]
    mine = pl.ds(pl.multiple_of(c * HB, HB), HB)

    def act_slot(r, o, h):
        return act_all.at[r, ARRIVALS.index((o, h)), :, mine]

    def act_send(r, name, o, h, axis_to, to_o):
        send(("a", r, name), act_slot(r, o, h), act_slot(r, to_o, h), "tpw", axis_to)

    def act_first(r, h):
        pre = trees[r][3](h)
        act = 0.5 * pre * (1.0 + lax.erf(pre * (2.0 ** -0.5)))
        act_all[r, ARRIVALS.index((0, h)), :, mine] = act.astype(BF16)
        if h == 0:
            act_send(r, "1r", 0, 0, right, 3)
        else:
            act_send(r, "1l", 0, 1, left, 1)
        act_send(r, ("s", 0, h), 0, h, sib, 0)

    def act_second(r):
        act_send(r, "2r", 0, 1, right, 3)
        act_send(r, "2l", 0, 0, left, 1)

    def act_third(r):
        arrived(("a", r, "1r"))
        act_send(r, "3r", 3, 0, right, 2)
        act_send(r, ("s", 3, 0), 3, 0, sib, 3)
        arrived(("a", r, "1l"))
        act_send(r, "3l", 1, 1, left, 2)
        act_send(r, ("s", 1, 1), 1, 1, sib, 1)

    def act_pass(r, name, o, h):
        arrived(("a", r, name))
        act_send(r, ("s", o, h), o, h, sib, o)

    def down_mm(r, i):
        o, h = ARRIVALS[i]
        arrived(("a", r, ("s", o, h)))
        if r == 0:
            loads[("down", i)].wait()
        part = dot(act_all[r, i], wdn_v[i])
        if i == 0:
            acc[r] = part
        else:
            acc[r] += part

    def rotary(t):
        swapped = jnp.where(first, pltpu.roll(t, 128 - half, 1), pltpu.roll(t, half, 1))
        return (t * cos_t + swapped * sin_t).astype(BF16).astype(F32)

    def attention():
        for g in range(G):
            qkv = q_total(g).astype(BF16).astype(F32)
            for t in range(QT):
                qrot[g, t * RB:(t + 1) * RB, :] = rotary(qkv[:, t * 128:(t + 1) * 128])
            last = qkv[:, QT * 128:]
            kv = jnp.where(plane < HD, rotary(last), last)
            kvrot[g] = kv
            knew_ref[:, g * HD:(g + 1) * HD] = kv[:, :HD].astype(BF16)
            vnew_ref[:, g * HD:(g + 1) * HD] = kv[:, HD:].astype(BF16)
        loads["k"].wait()
        loads["v"].wait()
        scale = HD ** -0.5
        when = lax.broadcasted_iota(jnp.int32, (2 * QT, L), 1)

        def row(b):
            for g in range(G):
                q8 = qrot[g, pl.ds(b, QT, stride=RB), :]
                q = jnp.concatenate([q8[:, :HD], q8[:, HD:]], axis=0)
                kv = kvrot[g, pl.ds(b, 1), :]
                s = dot(q.astype(BF16), k_v[b * G + g]) * scale
                s = jnp.where(when < pos_ref[b], s, -jnp.inf)
                sn = jnp.sum(q * kv[:, :HD], axis=1, keepdims=True) * scale
                m = jnp.maximum(jnp.max(s, axis=1, keepdims=True), sn)
                e = jnp.exp(s - m)
                en = jnp.exp(sn - m)
                rz = 1.0 / (jnp.sum(e, axis=1, keepdims=True) + en)
                wn = (en * rz).astype(BF16).astype(F32)
                ctx = dot((e * rz).astype(BF16), v_v[b * G + g], NT) + wn * kv[:, HD:]
                ctxs[g, pl.ds(b, QT, stride=RB), :] = jnp.concatenate([ctx[:QT], ctx[QT:]], axis=1)

        def rows(i, _):
            for j in range(4):
                row(i * 4 + j)
            return 0

        lax.fori_loop(0, RB // 4, rows, 0)
        for g in range(G):
            for t in range(QT):
                ctx_all[w, g, :, t * 128:(t + 1) * 128] = ctxs[g, t * RB:(t + 1) * RB, :].astype(BF16)

    def ctx_send(name, who, g, to):
        send(("c", name), ctx_all.at[who, g], ctx_all.at[who, g], "tpw", to)

    def ctx_first():
        ctx_send("1r", w, 0, right)
        ctx_send("1l", w, 1, left)
        ctx_send("2r", w, 1, right)
        ctx_send("2l", w, 0, left)
        for g in range(G):
            ctx_send(("s", 0, g), w, g, sib)

    def ctx_third():
        arrived(("c", "1r"))
        ctx_send("3r", left, 0, right)
        ctx_send(("s", 3, 0), left, 0, sib)
        arrived(("c", "1l"))
        ctx_send("3l", right, 1, left)
        ctx_send(("s", 1, 1), right, 1, sib)

    def ctx_rest():
        for name, who, o, g in (("2r", left, 3, 1), ("2l", right, 1, 0), ("3r", opp, 2, 0), ("3l", opp, 2, 1)):
            arrived(("c", name))
            ctx_send(("s", o, g), who, g, sib)

    def attn_mm():
        for o in range(NX):
            for g in range(G):
                arrived(("c", ("s", o, g)))
        loads["out"].wait()
        for g in range(G):
            n = QT * 128
            part = dot(ctx_all[:, g].reshape(R, n), wout_v[g * n:(g + 1) * n, :])
            for r in range(NG):
                acc[r] += part[r * RG:(r + 1) * RG]

    def y_scatter(r):
        ysend[r] = acc[r].astype(BF16)
        for i in range(1, NY):
            to = lax.rem(y + i, NY)
            rows = pl.ds(pl.multiple_of(to * RY, RY), RY)
            send(("y", r, i), ysend.at[r, rows], yrecv.at[r, i - 1], "tph", to)

    def y_gather(r):
        start = pl.multiple_of(y * RY, RY)
        tot = acc[r, pl.ds(start, RY), :]
        for i in range(1, NY):
            arrived(("y", r, i))
            tot = tot + yrecv[r, i - 1].astype(F32)
        rows = pl.ds(pl.multiple_of(r * RG + start, RY), RY)
        xout_ref[rows, :] = (x_v[rows, :].astype(F32) + tot).astype(BF16)
        for i in range(1, NY):
            send(("z", r, i), xout_ref.at[rows, :], xout_ref.at[rows, :], "tph", lax.rem(y + i, NY))

    qkv_mm(0)
    qkv_mm(1)
    up_mm(0, 0)
    up_mm(0, 1)
    for g in range(G):
        arrived(("qs", g))
    q1()
    q2()
    up_mm(0, 2)
    up_mm(0, 3)
    trees[0][0]()
    up_mm(0, 4)
    up_mm(0, 5)
    trees[0][1]()
    q3()
    up_mm(0, 6)
    up_mm(0, 7)
    up_mm(1, 0)
    up_mm(1, 1)
    trees[0][2]()
    up_mm(1, 2)
    up_mm(1, 3)
    trees[1][0]()
    up_mm(1, 4)
    up_mm(1, 5)
    trees[1][1]()
    up_mm(1, 6)
    up_mm(1, 7)
    act_first(0, 0)
    act_first(0, 1)
    trees[1][2]()
    act_second(0)
    attention()
    act_third(0)
    ctx_first()
    act_first(1, 0)
    act_first(1, 1)
    act_second(1)
    ctx_third()
    down_mm(0, 0)
    down_mm(0, 1)
    act_pass(0, "2r", 3, 1)
    act_pass(0, "2l", 1, 0)
    act_pass(0, "3r", 2, 0)
    act_pass(0, "3l", 2, 1)
    act_third(1)
    ctx_rest()
    for i in range(2, 8):
        down_mm(0, i)
    down_mm(1, 0)
    down_mm(1, 1)
    attn_mm()
    y_scatter(0)
    act_pass(1, "2r", 3, 1)
    act_pass(1, "2l", 1, 0)
    for i in range(2, 4):
        down_mm(1, i)
    act_pass(1, "3r", 2, 0)
    act_pass(1, "3l", 2, 1)
    y_gather(0)
    for i in range(4, 8):
        down_mm(1, i)
    y_scatter(1)
    y_gather(1)
    for r in range(NG):
        for i in range(1, NY):
            arrived(("z", r, i))
    for cp in sent:
        cp.wait_send()


def solution(mesh):
    W = mesh.shape["tpw"]
    NY = mesh.shape["tph"]
    if W != 8:
        raise ValueError("tpw")

    def local_layer(x_in, ln_attn, ln_mlp, w_qkv, w_out, w_up, w_down, k_cache, v_cache, positions):
        R, D = x_in.shape
        _, G, S, HD = w_qkv.shape
        F = w_up.shape[1]
        L = k_cache.shape[2]
        RB = R // W
        NX = W // 2
        NG = GROUPS_OF_ROWS
        RG = R // NG
        qw = S * HD
        cw = (S - 2) * HD
        QT = cw // 128
        HB = F // W // 2
        wqkv_t = jnp.transpose(w_qkv, (1, 2, 3, 0)).reshape(G * qw, D)
        k_t = jnp.swapaxes(k_cache, 2, 3).reshape(RB * G, HD, L)
        v_t = jnp.swapaxes(v_cache, 2, 3).reshape(RB * G, HD, L)
        n_messages = 7 + 2 + 6 + NG * 8 + NG * 6 + NG * 14 + 14 + NG * 6
        any_spec = pl.BlockSpec(memory_space=pl.ANY)
        vmem_spec = pl.BlockSpec(memory_space=pltpu.VMEM)
        x_out, k_new, v_new = pl.pallas_call(
            functools.partial(layer_kernel, W, NY),
            name="layer",
            out_shape=(
                jax.ShapeDtypeStruct((R, D), BF16),
                jax.ShapeDtypeStruct((RB, G * HD), BF16),
                jax.ShapeDtypeStruct((RB, G * HD), BF16),
            ),
            in_specs=[pl.BlockSpec(memory_space=pltpu.SMEM)] + [any_spec] * 9,
            out_specs=(vmem_spec,) * 3,
            scratch_shapes=[
                pltpu.VMEM((R, D), BF16),
                pltpu.VMEM((2, D), F32),
                pltpu.VMEM((2, D), F32),
                pltpu.VMEM((G, qw, D), BF16),
                pltpu.VMEM((G * cw, D), BF16),
                pltpu.VMEM((8, D, 2 * HB), BF16),
                pltpu.VMEM((8, 2 * HB, D), BF16),
                pltpu.VMEM((RB * G, HD, L), BF16),
                pltpu.VMEM((RB * G, HD, L), BF16),
                pltpu.VMEM((8, 128), F32),
                pltpu.VMEM((W - 1, 8, 128), F32),
                pltpu.VMEM((R, D), BF16),
                pltpu.VMEM((R, D), BF16),
                pltpu.VMEM((G, NX, 2, RB, qw), BF16),
                pltpu.VMEM((G, NX, RB, qw), BF16),
                pltpu.VMEM((6, RB, qw), BF16),
                pltpu.VMEM((6, RB, qw), BF16),
                pltpu.VMEM((G, QT * RB, 128), F32),
                pltpu.VMEM((G, RB, 128), F32),
                pltpu.VMEM((G, QT * RB, 128), F32),
                pltpu.VMEM((W, G, RB, cw), BF16),
                pltpu.VMEM((NG, 8, 2, RG, HB), BF16),
                pltpu.VMEM((NG, 8, RG, HB), BF16),
                pltpu.VMEM((NG, 6, RG, HB), BF16),
                pltpu.VMEM((NG, 6, RG, HB), BF16),
                pltpu.VMEM((NG, 8, RG, 2 * HB), BF16),
                pltpu.VMEM((NG, RG, D), F32),
                pltpu.VMEM((NG, RG, D), BF16),
                pltpu.VMEM((NG, NY - 1, RG // NY, D), BF16),
                pltpu.SemaphoreType.DMA((24,)),
                pltpu.SemaphoreType.DMA((n_messages,)),
                pltpu.SemaphoreType.DMA((n_messages,)),
            ],
            compiler_params=pltpu.CompilerParams(
                collective_id=0, has_side_effects=True, vmem_limit_bytes=VMEM_LIMIT
            ),
        )(
            positions, x_in, ln_attn, ln_mlp, wqkv_t, w_out.reshape(G * cw, D), w_up, w_down, k_t, v_t,
        )
        return x_out, k_new.reshape(RB, G, HD), v_new.reshape(RB, G, HD)

    cache_spec = P(("dp", "tpw"), "tph", None, None)
    new_spec = P(("dp", "tpw"), "tph", None)
    in_specs = (
        P("dp", "tpw"),
        P(None, "tpw"),
        P(None, "tpw"),
        P("tpw", "tph", None, None),
        P("tph", None, None, "tpw"),
        P("tpw", "tph"),
        P("tph", "tpw"),
        cache_spec,
        cache_spec,
        P(("dp", "tpw")),
    )
    out_specs = (P("dp", "tpw"), new_spec, new_spec)
    return jax.shard_map(local_layer, mesh=mesh, in_specs=in_specs, out_specs=out_specs, check_vma=False)
```

time: 185 us -> 66.7 us (0.36)
  the two profiles are of different devices: /device:TPU:97 before, /device:TPU:96 now
where the time goes in v1:
time: 66.7 us; the launch traced here: 66.5 us
  Pallas kernels  61.5 us (92%)
  local copies, waits for them, and re-layouts  4.39 us (7%)
    pallas_call x1, Pallas kernels, local_layer(): pl.pallas_call(functools.partial(layer_kernel, W, NY), name='layer', out_...  61.5 us
    reshape x2, local copies, waits for them, and re-layouts, local_layer(): return (x_out, k_new.reshape(RB, G, HD), v_new.reshape(RB, G, HD))  2.72 us
    unnamed x1, local copies, waits for them, and re-layouts  1.67 us

profile of v1, /device:TPU:96, one launch (start us, length us, event | category | flops | bytes accessed | tf_op | source)
XLA Modules:
  0.0 66.5 jit_solution(15489250232308965109)
XLA Ops:
  0.6 61.5 %layer.1 = (bf16[128,1024]{1,0:T(8,128)(2,1)}, bf16[16,128]{1,0:T(8,128)(2,1)}, bf16[16,128]{1,0:T(8,128)(2,1)}) custom-call(s32[16]{0:T(128)} %pos_ref.1, bf16[128,1024]{1,0:T(8,128)(2,1)} %x_hbm.1, f32[2,1024]{1,0:T(2,128)} %lna_hbm.1, f32[2,1024]{1,0:T(2,128)} %lnm_hbm.1, bf16[2304,1024]{1,0:T(8,128)(2,1)} %bitcast.10, bf16[2048,1024]{1,0:T(8,128)(2,1)} %bitcast.11, ...), custom_call_target="tpu_custom_call" | custom-call | tf_op jit(solution)/shard_map/layer/pallas_call | solution.py:444
  62.1 1.4 %reshape.28 = bf16[16,2,64]{2,1,0:T(2,128)(2,1)} reshape(bf16[16,128]{1,0:T(8,128)(2,1)} %get-tuple-element.7) | data formatting | bytes 8192 | tf_op jit(solution)/shard_map/reshape | solution.py:494
  63.5 1.4 %reshape.29 = bf16[16,2,64]{2,1,0:T(2,128)(2,1)} reshape(bf16[16,128]{1,0:T(8,128)(2,1)} %get-tuple-element.8) | data formatting | bytes 8192 | tf_op jit(solution)/shard_map/reshape | solution.py:494
  64.8 1.7 %copy.14 = bf16[128,1024]{1,0:T(8,128)(2,1)} copy(bf16[128,1024]{1,0:T(8,128)(2,1)} %get-tuple-element.12) | data formatting | bytes 524288

commit v2 on v1

--- a/solution.py
+++ b/solution.py
@@ -13,7 +13,7 @@
 MESH = pl.DeviceIdType.MESH
 F32 = jnp.float32
 BF16 = jnp.bfloat16
-VMEM_LIMIT = 67043328
+VMEM_LIMIT = 58 << 20
 GROUPS_OF_ROWS = 2
 NN = (((1,), (0,)), ((), ()))
 NT = (((1,), (1,)), ((), ()))
@@ -27,9 +27,9 @@
 
 def layer_kernel(
     W, NY,
-    pos_ref, x_hbm, lna_hbm, lnm_hbm, wqkv_hbm, wout_hbm, wup_hbm, wdn_hbm, k_hbm, v_hbm,
+    pos_hbm, x_hbm, lna_hbm, lnm_hbm, wqkv_hbm, wout_hbm, wup_hbm, wdn_hbm, k_hbm, v_hbm,
     xout_ref, knew_ref, vnew_ref,
-    x_v, lna_v, lnm_v, wqkv_v, wout_v, wup_v, wdn_v, k_v, v_v,
+    pos_ref, x_v, lna_v, lnm_v, wqkv_v, wout_v, wup_v, wdn_v, k_v, v_v,
     stat_send, stat_recv, ha_v, hm_v,
     qpart, qsib, qsend, qrecv, qrot, kvrot, ctxs, ctx_all,
     upart, usib, usend, urecv, act_all, acc, ysend, yrecv,
@@ -67,6 +67,7 @@
         loads[name] = cp
 
     load("x", x_hbm, x_v)
+    load("pos", pos_hbm, pos_ref)
     load("lna", lna_hbm, lna_v)
     load("lnm", lnm_hbm, lnm_v)
     qw = wqkv_v.shape[1]
@@ -114,6 +115,7 @@
     for i in range(1, W):
         send(("stat", i), stat_send, stat_recv.at[i - 1], "tpw", lax.rem(w + i, W))
 
+    loads["pos"].wait()
     prow = lax.broadcasted_iota(jnp.int32, (RB, 128), 0)
     plane = lax.broadcasted_iota(jnp.int32, (RB, 128), 1)
     pos = jnp.zeros((RB, 128), jnp.int32)
@@ -404,16 +406,24 @@
         down_mm(1, i)
     act_pass(1, "3r", 2, 0)
     act_pass(1, "3l", 2, 1)
-    y_gather(0)
     for i in range(4, 8):
         down_mm(1, i)
     y_scatter(1)
+    y_gather(0)
     y_gather(1)
     for r in range(NG):
         for i in range(1, NY):
             arrived(("z", r, i))
     for cp in sent:
         cp.wait_send()
+
+
+def finish_kernel(x_ref, k_ref, v_ref, xout_ref, knew_ref, vnew_ref):
+    xout_ref[...] = x_ref[...]
+    hd = knew_ref.shape[2]
+    for g in range(knew_ref.shape[1]):
+        knew_ref[:, g, :] = k_ref[:, g * hd:(g + 1) * hd]
+        vnew_ref[:, g, :] = v_ref[:, g * hd:(g + 1) * hd]
 
 
 def solution(mesh):
@@ -445,13 +455,14 @@
             functools.partial(layer_kernel, W, NY),
             name="layer",
             out_shape=(
-                jax.ShapeDtypeStruct((R, D), BF16),
-                jax.ShapeDtypeStruct((RB, G * HD), BF16),
-                jax.ShapeDtypeStruct((RB, G * HD), BF16),
+                pltpu.VMEM((R, D), BF16),
+                pltpu.VMEM((RB, G * HD), BF16),
+                pltpu.VMEM((RB, G * HD), BF16),
             ),
-            in_specs=[pl.BlockSpec(memory_space=pltpu.SMEM)] + [any_spec] * 9,
+            in_specs=[any_spec] * 10,
             out_specs=(vmem_spec,) * 3,
             scratch_shapes=[
+                pltpu.SMEM((RB,), jnp.int32),
                 pltpu.VMEM((R, D), BF16),
                 pltpu.VMEM((2, D), F32),
                 pltpu.VMEM((2, D), F32),
@@ -481,7 +492,7 @@
                 pltpu.VMEM((NG, RG, D), F32),
                 pltpu.VMEM((NG, RG, D), BF16),
                 pltpu.VMEM((NG, NY - 1, RG // NY, D), BF16),
-                pltpu.SemaphoreType.DMA((24,)),
+                pltpu.SemaphoreType.DMA((32,)),
                 pltpu.SemaphoreType.DMA((n_messages,)),
                 pltpu.SemaphoreType.DMA((n_messages,)),
             ],
@@ -491,7 +502,17 @@
         )(
             positions, x_in, ln_attn, ln_mlp, wqkv_t, w_out.reshape(G * cw, D), w_up, w_down, k_t, v_t,
         )
-        return x_out, k_new.reshape(RB, G, HD), v_new.reshape(RB, G, HD)
+        return pl.pallas_call(
+            finish_kernel,
+            name="finish",
+            out_shape=(
+                jax.ShapeDtypeStruct((R, D), BF16),
+                jax.ShapeDtypeStruct((RB, G, HD), BF16),
+                jax.ShapeDtypeStruct((RB, G, HD), BF16),
+            ),
+            in_specs=[vmem_spec] * 3,
+            out_specs=(vmem_spec,) * 3,
+        )(*(pltpu.with_memory_space_constraint(a, pltpu.VMEM) for a in (x_out, k_new, v_new)))
 
     cache_spec = P(("dp", "tpw"), "tph", None, None)
     new_spec = P(("dp", "tpw"), "tph", None)

time: 66.7 us -> 58.5 us (0.88)
  the two profiles are of different devices: /device:TPU:96 before, /device:TPU:97 now
where the time goes in v2:
time: 58.5 us; the launch traced here: 58.4 us
  Pallas kernels  57.8 us (99%)
  between operations  0.64 us (1%)
    pallas_call x1, Pallas kernels, local_layer(): pl.pallas_call(functools.partial(layer_kernel, W, NY), name='layer', out_...  57 us

profile of v2, /device:TPU:97, one launch (start us, length us, event | category | flops | bytes accessed | tf_op | source)
XLA Modules:
  0.0 58.4 jit_solution(6991168573237919432)
XLA Ops:
  0.6 57.0 %layer.1 = (bf16[128,1024]{1,0:T(8,128)(2,1)S(1)}, bf16[16,128]{1,0:T(8,128)(2,1)S(1)}, bf16[16,128]{1,0:T(8,128)(2,1)S(1)}) custom-call(s32[16]{0:T(128)} %pos_hbm.1, bf16[128,1024]{1,0:T(8,128)(2,1)} %x_hbm.1, f32[2,1024]{1,0:T(2,128)} %lna_hbm.1, f32[2,1024]{1,0:T(2,128)} %lnm_hbm.1, bf16[2304,1024]{1,0:T(8,128)(2,1)} %bitcast.10, ...), custom_call_target="tpu_custom_call" | custom-call | tf_op jit(solution)/shard_map/layer/pallas_call | solution.py:454
  57.7 0.7 %finish.1 = (bf16[128,1024]{1,0:T(8,128)(2,1)}, bf16[16,2,64]{2,1,0:T(2,128)(2,1)}, bf16[16,2,64]{2,1,0:T(2,128)(2,1)}) custom-call(bf16[128,1024]{1,0:T(8,128)(2,1)S(1)} %get-tuple-element.6.x_ref, bf16[16,128]{1,0:T(8,128)(2,1)S(1)} %get-tuple-element.7.k_ref, bf16[16,128]{1,0:T(8,128)(2,1)S(1)} %get-tuple-element.8.v_ref), custom_call_target="tpu_custom_call" | custom-call | tf_op jit(solution)/shard_map/finish/pallas_call | solution.py:505

commit v3 on v2

--- a/solution.py
+++ b/solution.py
@@ -19,6 +19,25 @@
 NT = (((1,), (1,)), ((), ()))
 PIECES = ((2, 0), (2, 1), (1, 1), (3, 0), (1, 0), (3, 1), (0, 0), (0, 1))
 ARRIVALS = ((0, 0), (0, 1), (3, 0), (1, 1), (3, 1), (1, 0), (2, 0), (2, 1))
+
+ORDER = (
+    ("qmm", 1), ("qmm", 0), ("umm", 0, 1), ("umm", 0, 2), ("qm", "2r"), ("qm", "1l"),
+    ("umm", 0, 0), ("umm", 0, 5), ("um", 0, "1l"), ("qm", "1r"), ("umm", 1, 1), ("um", 0, "2r"),
+    ("umm", 1, 3), ("um", 0, "1r"), ("umm", 1, 4), ("umm", 1, 5), ("umm", 0, 4), ("um", 1, "2l"),
+    ("umm", 1, 0), ("um", 1, "1l"), ("umm", 0, 6), ("umm", 0, 7), ("umm", 1, 6), ("qm", "3l"),
+    ("um", 1, "1r"), ("qm", "2l"), ("umm", 1, 2), ("umm", 0, 3), ("qm", "3r"), ("umm", 1, 7),
+    ("um", 0, "3l"), ("um", 1, "2r"), ("um", 0, "2l"), ("um", 0, "3r"), ("um", 1, "3l"), ("um", 1, "3r"),
+    ("qt", 1), ("att", 1), ("c", "1l"), ("qt", 0), ("c", "2r"), ("att", 0),
+    ("c", "2l"), ("c", "1r"), ("a", 0, "1"), ("a", 0, "2r"), ("dmm", 0, 1), ("a", 0, "0"),
+    ("a", 0, "2l"), ("a", 1, "0"), ("a", 1, "1"), ("a", 1, "2r"), ("a", 1, "2l"), ("dmm", 0, 0),
+    ("pc", "2r"), ("c", "3l"), ("dmm", 1, 0), ("c", "3r"), ("dmm", 1, 1), ("pc", "2l"),
+    ("ap", 0, "2r"), ("a", 0, "3l"), ("dmm", 0, 4), ("a", 0, "3r"), ("dmm", 0, 3), ("ap", 0, "2l"),
+    ("dmm", 0, 2), ("a", 1, "3r"), ("dmm", 0, 5), ("a", 1, "3l"), ("dmm", 1, 2), ("ap", 1, "2r"),
+    ("dmm", 1, 3), ("ap", 1, "2l"), ("pc", "3r"), ("dmm", 1, 4), ("dmm", 1, 5), ("pc", "3l"),
+    ("ap", 0, "3r"), ("ap", 0, "3l"), ("amm",), ("dmm", 0, 6), ("ap", 1, "3r"), ("dmm", 0, 7),
+    ("ysc", 0), ("ap", 1, "3l"), ("dmm", 1, 6), ("dmm", 1, 7), ("ysc", 1), ("yga", 0),
+    ("yga", 1),
+)
 
 
 def dot(a, b, dims=NN):
@@ -59,6 +78,12 @@
     def chip(o):
         return lax.rem(x + o, NX)
 
+    barrier = pltpu.get_barrier_semaphore()
+    for i in range(1, W):
+        pl.semaphore_signal(barrier, inc=1, device_id={"tpw": lax.rem(w + i, W)}, device_id_type=MESH)
+    for i in range(1, NY):
+        pl.semaphore_signal(barrier, inc=1, device_id={"tph": lax.rem(y + i, NY)}, device_id_type=MESH)
+
     loads = {}
 
     def load(name, src, dst):
@@ -83,12 +108,6 @@
         row = pl.multiple_of((chip(o) * 2 + h) * 2 * HB, 2 * HB)
         load(("down", i), wdn_hbm.at[pl.ds(row, 2 * HB), :], wdn_v.at[i])
 
-    barrier = pltpu.get_barrier_semaphore()
-    for i in range(1, W):
-        pl.semaphore_signal(barrier, inc=1, device_id={"tpw": lax.rem(w + i, W)}, device_id_type=MESH)
-    for i in range(1, NY):
-        pl.semaphore_signal(barrier, inc=1, device_id={"tph": lax.rem(y + i, NY)}, device_id_type=MESH)
-
     sent = []
     messages = {}
 
@@ -102,8 +121,17 @@
         sent.append(cp)
         messages[name] = cp
 
+    seen = set()
+
     def arrived(name):
-        messages[name].wait_recv()
+        if name not in seen:
+            seen.add(name)
+            messages[name].wait_recv()
+
+    def need(name):
+        if name not in seen:
+            seen.add(name)
+            loads[name].wait()
 
     loads["x"].wait()
     xf = x_v[...].astype(F32)
@@ -143,200 +171,201 @@
     ha_v[...] = (cen * lna_v[0:1, :] + lna_v[1:2, :]).astype(BF16)
     hm_v[...] = (cen * lnm_v[0:1, :] + lnm_v[1:2, :]).astype(BF16)
 
-    def tree(tag, own, stage, landing):
-        def m1():
-            stage[0] = own(2, 0).astype(BF16)
-            send((tag, 0), stage.at[0], landing.at[0], "tpw", right)
-            stage[1] = own(2, 1).astype(BF16)
-            send((tag, 1), stage.at[1], landing.at[1], "tpw", left)
-
-        def m2():
-            stage[2] = own(1, 1).astype(BF16)
-            send((tag, 2), stage.at[2], landing.at[2], "tpw", right)
-            stage[3] = own(3, 0).astype(BF16)
-            send((tag, 3), stage.at[3], landing.at[3], "tpw", left)
-
-        def m3():
-            arrived((tag, 0))
-            stage[4] = (own(1, 0) + landing[0].astype(F32)).astype(BF16)
-            send((tag, 4), stage.at[4], landing.at[4], "tpw", right)
-            arrived((tag, 1))
-            stage[5] = (own(3, 1) + landing[1].astype(F32)).astype(BF16)
-            send((tag, 5), stage.at[5], landing.at[5], "tpw", left)
-
-        def total(h):
-            a, b = ((3, 4), (2, 5))[h]
-            arrived((tag, a))
-            arrived((tag, b))
-            return own(0, h) + landing[a].astype(F32) + landing[b].astype(F32)
-
-        return m1, m2, m3, total
-
-    def qkv_mm(g):
-        loads[("qkv", g)].wait()
+    legs = {
+        "1r": (0, 2, 0, None, right), "1l": (1, 2, 1, None, left),
+        "2r": (2, 1, 1, None, right), "2l": (3, 3, 0, None, left),
+        "3r": (4, 1, 0, 0, right), "3l": (5, 3, 1, 1, left),
+    }
+
+    def leg(tag, key, own, stage, landing):
+        i, o, h, add, to = legs[key]
+        val = own(o, h)
+        if add is not None:
+            arrived((tag, add))
+            val = val + landing[add].astype(F32)
+        stage[i] = val.astype(BF16)
+        send((tag, i), stage.at[i], landing.at[i], "tpw", to)
+
+    def total(tag, h, own, landing):
+        val = own(0, h)
+        for i in ((3, 4), (2, 5))[h]:
+            arrived((tag, i))
+            val = val + landing[i].astype(F32)
+        return val
+
+    def qmm(g):
+        need(("qkv", g))
         part = dot(ha_v[...], wqkv_v[g], NT).astype(BF16)
         qpart[g] = part.reshape(NX, 2, RB, qw)
         send(("qs", g), qpart.at[g, :, 1 - c], qsib.at[g], "tpw", sib)
 
     def qkv_own(o, g):
+        arrived(("qs", g))
         return qpart[g, chip(o), c].astype(F32) + qsib[g, chip(o)].astype(F32)
 
-    q1, q2, q3, q_total = tree("q", qkv_own, qsend, qrecv)
-
-    def up_mm(r, i):
-        if r == 0:
-            loads[("up", i)].wait()
+    def qm(key):
+        leg("q", key, qkv_own, qsend, qrecv)
+
+    def umm(r, i):
+        need(("up", i))
         hm = hm_v[r * RG:(r + 1) * RG, :]
         for k in range(2):
             upart[r, i, k] = dot(hm, wup_v[i, :, k * HB:(k + 1) * HB]).astype(BF16)
         send(("us", r, i), upart.at[r, i, 1 - c], usib.at[r, i], "tpw", sib)
 
-    def up_tree(r):
-        waited = set()
-
+    def up_own(r):
         def own(o, h):
             i = PIECES.index((o, h))
-            if i not in waited:
-                arrived(("us", r, i))
-                waited.add(i)
+            arrived(("us", r, i))
             return upart[r, i, c].astype(F32) + usib[r, i].astype(F32)
 
-        return tree(("u", r), own, usend.at[r], urecv.at[r])
-
-    trees = [up_tree(r) for r in range(NG)]
+        return own
+
+    def um(r, key):
+        leg(("u", r), key, up_own(r), usend.at[r], urecv.at[r])
+
     mine = pl.ds(pl.multiple_of(c * HB, HB), HB)
 
-    def act_slot(r, o, h):
-        return act_all.at[r, ARRIVALS.index((o, h)), :, mine]
-
-    def act_send(r, name, o, h, axis_to, to_o):
-        send(("a", r, name), act_slot(r, o, h), act_slot(r, to_o, h), "tpw", axis_to)
-
-    def act_first(r, h):
-        pre = trees[r][3](h)
-        act = 0.5 * pre * (1.0 + lax.erf(pre * (2.0 ** -0.5)))
-        act_all[r, ARRIVALS.index((0, h)), :, mine] = act.astype(BF16)
-        if h == 0:
-            act_send(r, "1r", 0, 0, right, 3)
+    def act_send(r, name, o, h, to, to_o):
+        src = act_all.at[r, ARRIVALS.index((o, h)), :, mine]
+        dst = act_all.at[r, ARRIVALS.index((to_o, h)), :, mine]
+        send(("a", r, name), src, dst, "tpw", to)
+
+    def act(r, key):
+        if key in ("0", "1"):
+            h = int(key)
+            pre = total(("u", r), h, up_own(r), urecv.at[r])
+            val = 0.5 * pre * (1.0 + lax.erf(pre * (2.0 ** -0.5)))
+            act_all[r, ARRIVALS.index((0, h)), :, mine] = val.astype(BF16)
+            if h == 0:
+                act_send(r, "1r", 0, 0, right, 3)
+            else:
+                act_send(r, "1l", 0, 1, left, 1)
+            act_send(r, ("s", 0, h), 0, h, sib, 0)
+        elif key == "2r":
+            act_send(r, "2r", 0, 1, right, 3)
+        elif key == "2l":
+            act_send(r, "2l", 0, 0, left, 1)
+        elif key == "3r":
+            arrived(("a", r, "1r"))
+            act_send(r, "3r", 3, 0, right, 2)
+            act_send(r, ("s", 3, 0), 3, 0, sib, 3)
         else:
-            act_send(r, "1l", 0, 1, left, 1)
-        act_send(r, ("s", 0, h), 0, h, sib, 0)
-
-    def act_second(r):
-        act_send(r, "2r", 0, 1, right, 3)
-        act_send(r, "2l", 0, 0, left, 1)
-
-    def act_third(r):
-        arrived(("a", r, "1r"))
-        act_send(r, "3r", 3, 0, right, 2)
-        act_send(r, ("s", 3, 0), 3, 0, sib, 3)
-        arrived(("a", r, "1l"))
-        act_send(r, "3l", 1, 1, left, 2)
-        act_send(r, ("s", 1, 1), 1, 1, sib, 1)
-
-    def act_pass(r, name, o, h):
-        arrived(("a", r, name))
+            arrived(("a", r, "1l"))
+            act_send(r, "3l", 1, 1, left, 2)
+            act_send(r, ("s", 1, 1), 1, 1, sib, 1)
+
+    def ap(r, key):
+        o, h = {"2r": (3, 1), "2l": (1, 0), "3r": (2, 0), "3l": (2, 1)}[key]
+        arrived(("a", r, key))
         act_send(r, ("s", o, h), o, h, sib, o)
 
-    def down_mm(r, i):
+    begun = set()
+
+    def accumulate(r, part):
+        if r in begun:
+            acc[r] += part
+        else:
+            acc[r] = part
+            begun.add(r)
+
+    def dmm(r, i):
         o, h = ARRIVALS[i]
         arrived(("a", r, ("s", o, h)))
-        if r == 0:
-            loads[("down", i)].wait()
-        part = dot(act_all[r, i], wdn_v[i])
-        if i == 0:
-            acc[r] = part
-        else:
-            acc[r] += part
+        need(("down", i))
+        accumulate(r, dot(act_all[r, i], wdn_v[i]))
+
+    scale = HD ** -0.5
+    when = lax.broadcasted_iota(jnp.int32, (2 * QT, L), 1)
 
     def rotary(t):
         swapped = jnp.where(first, pltpu.roll(t, 128 - half, 1), pltpu.roll(t, half, 1))
         return (t * cos_t + swapped * sin_t).astype(BF16).astype(F32)
 
-    def attention():
-        for g in range(G):
-            qkv = q_total(g).astype(BF16).astype(F32)
-            for t in range(QT):
-                qrot[g, t * RB:(t + 1) * RB, :] = rotary(qkv[:, t * 128:(t + 1) * 128])
-            last = qkv[:, QT * 128:]
-            kv = jnp.where(plane < HD, rotary(last), last)
-            kvrot[g] = kv
-            knew_ref[:, g * HD:(g + 1) * HD] = kv[:, :HD].astype(BF16)
-            vnew_ref[:, g * HD:(g + 1) * HD] = kv[:, HD:].astype(BF16)
-        loads["k"].wait()
-        loads["v"].wait()
-        scale = HD ** -0.5
-        when = lax.broadcasted_iota(jnp.int32, (2 * QT, L), 1)
+    def qt(g):
+        qkv = total("q", g, qkv_own, qrecv).astype(BF16).astype(F32)
+        for t in range(QT):
+            qrot[g, t * RB:(t + 1) * RB, :] = rotary(qkv[:, t * 128:(t + 1) * 128])
+        last = qkv[:, QT * 128:]
+        kv = jnp.where(plane < HD, rotary(last), last)
+        kvrot[g] = kv
+        knew_ref[:, g * HD:(g + 1) * HD] = kv[:, :HD].astype(BF16)
+        vnew_ref[:, g * HD:(g + 1) * HD] = kv[:, HD:].astype(BF16)
+
+    def att(g):
+        need("k")
+        need("v")
 
         def row(b):
-            for g in range(G):
-                q8 = qrot[g, pl.ds(b, QT, stride=RB), :]
-                q = jnp.concatenate([q8[:, :HD], q8[:, HD:]], axis=0)
-                kv = kvrot[g, pl.ds(b, 1), :]
-                s = dot(q.astype(BF16), k_v[b * G + g]) * scale
-                s = jnp.where(when < pos_ref[b], s, -jnp.inf)
-                sn = jnp.sum(q * kv[:, :HD], axis=1, keepdims=True) * scale
-                m = jnp.maximum(jnp.max(s, axis=1, keepdims=True), sn)
-                e = jnp.exp(s - m)
-                en = jnp.exp(sn - m)
-                rz = 1.0 / (jnp.sum(e, axis=1, keepdims=True) + en)
-                wn = (en * rz).astype(BF16).astype(F32)
-                ctx = dot((e * rz).astype(BF16), v_v[b * G + g], NT) + wn * kv[:, HD:]
-                ctxs[g, pl.ds(b, QT, stride=RB), :] = jnp.concatenate([ctx[:QT], ctx[QT:]], axis=1)
+            q8 = qrot[g, pl.ds(b, QT, stride=RB), :]
+            q = jnp.concatenate([q8[:, :HD], q8[:, HD:]], axis=0)
+            kv = kvrot[g, pl.ds(b, 1), :]
+            s = dot(q.astype(BF16), k_v[b * G + g]) * scale
+            s = jnp.where(when < pos_ref[b], s, -jnp.inf)
+            sn = jnp.sum(q * kv[:, :HD], axis=1, keepdims=True) * scale
+            m = jnp.maximum(jnp.max(s, axis=1, keepdims=True), sn)
+            e = jnp.exp(s - m)
+            en = jnp.exp(sn - m)
+            rz = 1.0 / (jnp.sum(e, axis=1, keepdims=True) + en)
+            wn = (en * rz).astype(BF16).astype(F32)
+            ctx = dot((e * rz).astype(BF16), v_v[b * G + g], NT) + wn * kv[:, HD:]
+            ctxs[g, pl.ds(b, QT, stride=RB), :] = jnp.concatenate([ctx[:QT], ctx[QT:]], axis=1)
 
         def rows(i, _):
-            for j in range(4):
-                row(i * 4 + j)
+            for j in range(8):
+                row(i * 8 + j)
             return 0
 
-        lax.fori_loop(0, RB // 4, rows, 0)
-        for g in range(G):
-            for t in range(QT):
-                ctx_all[w, g, :, t * 128:(t + 1) * 128] = ctxs[g, t * RB:(t + 1) * RB, :].astype(BF16)
+        lax.fori_loop(0, RB // 8, rows, 0)
+        for t in range(QT):
+            ctx_all[w, g, :, t * 128:(t + 1) * 128] = ctxs[g, t * RB:(t + 1) * RB, :].astype(BF16)
+        send(("c", ("s", 0, g)), ctx_all.at[w, g], ctx_all.at[w, g], "tpw", sib)
 
     def ctx_send(name, who, g, to):
         send(("c", name), ctx_all.at[who, g], ctx_all.at[who, g], "tpw", to)
 
-    def ctx_first():
-        ctx_send("1r", w, 0, right)
-        ctx_send("1l", w, 1, left)
-        ctx_send("2r", w, 1, right)
-        ctx_send("2l", w, 0, left)
-        for g in range(G):
-            ctx_send(("s", 0, g), w, g, sib)
-
-    def ctx_third():
-        arrived(("c", "1r"))
-        ctx_send("3r", left, 0, right)
-        ctx_send(("s", 3, 0), left, 0, sib)
-        arrived(("c", "1l"))
-        ctx_send("3l", right, 1, left)
-        ctx_send(("s", 1, 1), right, 1, sib)
-
-    def ctx_rest():
-        for name, who, o, g in (("2r", left, 3, 1), ("2l", right, 1, 0), ("3r", opp, 2, 0), ("3l", opp, 2, 1)):
-            arrived(("c", name))
-            ctx_send(("s", o, g), who, g, sib)
-
-    def attn_mm():
+    def ctx(key):
+        if key == "1r":
+            ctx_send("1r", w, 0, right)
+        elif key == "1l":
+            ctx_send("1l", w, 1, left)
+        elif key == "2r":
+            ctx_send("2r", w, 1, right)
+        elif key == "2l":
+            ctx_send("2l", w, 0, left)
+        elif key == "3r":
+            arrived(("c", "1r"))
+            ctx_send("3r", left, 0, right)
+            ctx_send(("s", 3, 0), left, 0, sib)
+        else:
+            arrived(("c", "1l"))
+            ctx_send("3l", right, 1, left)
+            ctx_send(("s", 1, 1), right, 1, sib)
+
+    def pc(key):
+        who, o, g = {"2r": (left, 3, 1), "2l": (right, 1, 0), "3r": (opp, 2, 0), "3l": (opp, 2, 1)}[key]
+        arrived(("c", key))
+        ctx_send(("s", o, g), who, g, sib)
+
+    def amm():
         for o in range(NX):
             for g in range(G):
                 arrived(("c", ("s", o, g)))
-        loads["out"].wait()
+        need("out")
+        n = QT * 128
         for g in range(G):
-            n = QT * 128
             part = dot(ctx_all[:, g].reshape(R, n), wout_v[g * n:(g + 1) * n, :])
             for r in range(NG):
-                acc[r] += part[r * RG:(r + 1) * RG]
-
-    def y_scatter(r):
+                accumulate(r, part[r * RG:(r + 1) * RG])
+
+    def ysc(r):
         ysend[r] = acc[r].astype(BF16)
-        for i in range(1, NY):
+        for i in (2, 1, 3):
             to = lax.rem(y + i, NY)
             rows = pl.ds(pl.multiple_of(to * RY, RY), RY)
             send(("y", r, i), ysend.at[r, rows], yrecv.at[r, i - 1], "tph", to)
 
-    def y_gather(r):
+    def yga(r):
         start = pl.multiple_of(y * RY, RY)
         tot = acc[r, pl.ds(start, RY), :]
         for i in range(1, NY):
@@ -344,76 +373,17 @@
             tot = tot + yrecv[r, i - 1].astype(F32)
         rows = pl.ds(pl.multiple_of(r * RG + start, RY), RY)
         xout_ref[rows, :] = (x_v[rows, :].astype(F32) + tot).astype(BF16)
-        for i in range(1, NY):
+        for i in (2, 1, 3):
             send(("z", r, i), xout_ref.at[rows, :], xout_ref.at[rows, :], "tph", lax.rem(y + i, NY))
 
-    qkv_mm(0)
-    qkv_mm(1)
-    up_mm(0, 0)
-    up_mm(0, 1)
-    for g in range(G):
-        arrived(("qs", g))
-    q1()
-    q2()
-    up_mm(0, 2)
-    up_mm(0, 3)
-    trees[0][0]()
-    up_mm(0, 4)
-    up_mm(0, 5)
-    trees[0][1]()
-    q3()
-    up_mm(0, 6)
-    up_mm(0, 7)
-    up_mm(1, 0)
-    up_mm(1, 1)
-    trees[0][2]()
-    up_mm(1, 2)
-    up_mm(1, 3)
-    trees[1][0]()
-    up_mm(1, 4)
-    up_mm(1, 5)
-    trees[1][1]()
-    up_mm(1, 6)
-    up_mm(1, 7)
-    act_first(0, 0)
-    act_first(0, 1)
-    trees[1][2]()
-    act_second(0)
-    attention()
-    act_third(0)
-    ctx_first()
-    act_first(1, 0)
-    act_first(1, 1)
-    act_second(1)
-    ctx_third()
-    down_mm(0, 0)
-    down_mm(0, 1)
-    act_pass(0, "2r", 3, 1)
-    act_pass(0, "2l", 1, 0)
-    act_pass(0, "3r", 2, 0)
-    act_pass(0, "3l", 2, 1)
-    act_third(1)
-    ctx_rest()
-    for i in range(2, 8):
-        down_mm(0, i)
-    down_mm(1, 0)
-    down_mm(1, 1)
-    attn_mm()
-    y_scatter(0)
-    act_pass(1, "2r", 3, 1)
-    act_pass(1, "2l", 1, 0)
-    for i in range(2, 4):
-        down_mm(1, i)
-    act_pass(1, "3r", 2, 0)
-    act_pass(1, "3l", 2, 1)
-    for i in range(4, 8):
-        down_mm(1, i)
-    y_scatter(1)
-    y_gather(0)
-    y_gather(1)
-    for r in range(NG):
-        for i in range(1, NY):
-            arrived(("z", r, i))
+    steps = {
+        "qmm": qmm, "qm": qm, "umm": umm, "um": um, "a": act, "ap": ap, "dmm": dmm, "qt": qt, "att": att,
+        "c": ctx, "pc": pc, "amm": amm, "ysc": ysc, "yga": yga,
+    }
+    for step in ORDER:
+        steps[step[0]](*step[1:])
+    for name in messages:
+        arrived(name)
     for cp in sent:
         cp.wait_send()
 

time: 58.5 us -> 56 us (0.957)
  Pallas kernels: 57.8 us -> 55.3 us
    pallas_call x1, Pallas kernels: 57 us -> 54.6 us  [local_layer(): pl.pallas_call(functools.partial(layer_kernel, W, NY), name='layer', out_...]
where the time goes in v3:
time: 56 us; the launch traced here: 55.9 us
  Pallas kernels  55.3 us (99%)
  between operations  0.64 us (1%)
    pallas_call x1, Pallas kernels, local_layer(): pl.pallas_call(functools.partial(layer_kernel, W, NY), name='layer', out_...  54.6 us

profile of v3, /device:TPU:97, one launch (start us, length us, event | category | flops | bytes accessed | tf_op | source)
XLA Modules:
  0.0 55.9 jit_solution(7762294738636362495)
XLA Ops:
  0.6 54.6 %layer.1 = (bf16[128,1024]{1,0:T(8,128)(2,1)S(1)}, bf16[16,128]{1,0:T(8,128)(2,1)S(1)}, bf16[16,128]{1,0:T(8,128)(2,1)S(1)}) custom-call(s32[16]{0:T(128)} %pos_hbm.1, bf16[128,1024]{1,0:T(8,128)(2,1)} %x_hbm.1, f32[2,1024]{1,0:T(2,128)} %lna_hbm.1, f32[2,1024]{1,0:T(2,128)} %lnm_hbm.1, bf16[2304,1024]{1,0:T(8,128)(2,1)} %bitcast.10, ...), custom_call_target="tpu_custom_call" | custom-call | tf_op jit(solution)/shard_map/layer/pallas_call | solution.py:424
  55.2 0.7 %finish.1 = (bf16[128,1024]{1,0:T(8,128)(2,1)}, bf16[16,2,64]{2,1,0:T(2,128)(2,1)}, bf16[16,2,64]{2,1,0:T(2,128)(2,1)}) custom-call(bf16[128,1024]{1,0:T(8,128)(2,1)S(1)} %get-tuple-element.6.x_ref, bf16[16,128]{1,0:T(8,128)(2,1)S(1)} %get-tuple-element.7.k_ref, bf16[16,128]{1,0:T(8,128)(2,1)S(1)} %get-tuple-element.8.v_ref), custom_call_target="tpu_custom_call" | custom-call | tf_op jit(solution)/shard_map/finish/pallas_call | solution.py:475

commit v4 on v3

--- a/solution.py
+++ b/solution.py
@@ -20,6 +20,12 @@
 PIECES = ((2, 0), (2, 1), (1, 1), (3, 0), (1, 0), (3, 1), (0, 0), (0, 1))
 ARRIVALS = ((0, 0), (0, 1), (3, 0), (1, 1), (3, 1), (1, 0), (2, 0), (2, 1))
 
+LOADS = (
+    (("up", 1), ("up", 2),),
+    (("up", 0), ("up", 5), ("up", 3),),
+    (("up", 4), ("up", 6), ("up", 7),),
+    (("kv",), ("down", 1), ("down", 0), ("out",), ("down", 4), ("down", 3), ("down", 2), ("down", 5), ("down", 6), ("down", 7),),
+)
 ORDER = (
     ("qmm", 1), ("qmm", 0), ("umm", 0, 1), ("umm", 0, 2), ("qm", "2r"), ("qm", "1l"),
     ("umm", 0, 0), ("umm", 0, 5), ("um", 0, "1l"), ("qm", "1r"), ("umm", 1, 1), ("um", 0, "2r"),
@@ -91,22 +97,37 @@
         cp.start()
         loads[name] = cp
 
+    qw = wqkv_v.shape[1]
+
+    def load_up(i):
+        o, h = PIECES[i]
+        col = pl.multiple_of((chip(o) * 2 + h) * 2 * HB, 2 * HB)
+        load(("up", i), wup_hbm.at[:, pl.ds(col, 2 * HB)], wup_v.at[i])
+
+    def load_down(i):
+        o, h = ARRIVALS[i]
+        row = pl.multiple_of((chip(o) * 2 + h) * 2 * HB, 2 * HB)
+        load(("down", i), wdn_hbm.at[pl.ds(row, 2 * HB), :], wdn_v.at[i])
+
+    def ld(key, *index):
+        if key == "up":
+            load_up(*index)
+        elif key == "down":
+            load_down(*index)
+        elif key == "kv":
+            load("k", k_hbm, k_v)
+            load("v", v_hbm, v_v)
+        else:
+            load("out", wout_hbm, wout_v)
+
     load("x", x_hbm, x_v)
     load("pos", pos_hbm, pos_ref)
     load("lna", lna_hbm, lna_v)
     load("lnm", lnm_hbm, lnm_v)
-    qw = wqkv_v.shape[1]
     for g in range(G):
         load(("qkv", g), wqkv_hbm.at[pl.ds(g * qw, qw), :], wqkv_v.at[g])
-    for i, (o, h) in enumerate(PIECES):
-        col = pl.multiple_of((chip(o) * 2 + h) * 2 * HB, 2 * HB)
-        load(("up", i), wup_hbm.at[:, pl.ds(col, 2 * HB)], wup_v.at[i])
-    load("k", k_hbm, k_v)
-    load("v", v_hbm, v_v)
-    load("out", wout_hbm, wout_v)
-    for i, (o, h) in enumerate(ARRIVALS):
-        row = pl.multiple_of((chip(o) * 2 + h) * 2 * HB, 2 * HB)
-        load(("down", i), wdn_hbm.at[pl.ds(row, 2 * HB), :], wdn_v.at[i])
+    for step in LOADS[0]:
+        ld(*step)
 
     sent = []
     messages = {}
@@ -142,6 +163,9 @@
     pl.semaphore_wait(barrier, W - 1 + NY - 1)
     for i in range(1, W):
         send(("stat", i), stat_send, stat_recv.at[i - 1], "tpw", lax.rem(w + i, W))
+
+    for step in LOADS[1]:
+        ld(*step)
 
     loads["pos"].wait()
     prow = lax.broadcasted_iota(jnp.int32, (RB, 128), 0)
@@ -170,6 +194,9 @@
     cen = (x_v[...].astype(F32) - mean) * rstd
     ha_v[...] = (cen * lna_v[0:1, :] + lna_v[1:2, :]).astype(BF16)
     hm_v[...] = (cen * lnm_v[0:1, :] + lnm_v[1:2, :]).astype(BF16)
+
+    for step in LOADS[2]:
+        ld(*step)
 
     legs = {
         "1r": (0, 2, 0, None, right), "1l": (1, 2, 1, None, left),
@@ -380,8 +407,11 @@
         "qmm": qmm, "qm": qm, "umm": umm, "um": um, "a": act, "ap": ap, "dmm": dmm, "qt": qt, "att": att,
         "c": ctx, "pc": pc, "amm": amm, "ysc": ysc, "yga": yga,
     }
+    later = list(LOADS[3])
     for step in ORDER:
         steps[step[0]](*step[1:])
+        if later and step[0] == "umm":
+            ld(*later.pop(0))
     for name in messages:
         arrived(name)
     for cp in sent:

time: 56 us -> 56.1 us (level)
  no operation moved by 1% of the time
where the time goes in v4:
time: 56.1 us; the launch traced here: 56 us
  Pallas kernels  55.4 us (99%)
  between operations  0.64 us (1%)
    pallas_call x1, Pallas kernels, local_layer(): pl.pallas_call(functools.partial(layer_kernel, W, NY), name='layer', out_...  54.6 us

profile of v4, /device:TPU:97, one launch (start us, length us, event | category | flops | bytes accessed | tf_op | source)
XLA Modules:
  0.0 56.0 jit_solution(5200644546096534382)
XLA Ops:
  0.6 54.6 %layer.1 = (bf16[128,1024]{1,0:T(8,128)(2,1)S(1)}, bf16[16,128]{1,0:T(8,128)(2,1)S(1)}, bf16[16,128]{1,0:T(8,128)(2,1)S(1)}) custom-call(s32[16]{0:T(128)} %pos_hbm.1, bf16[128,1024]{1,0:T(8,128)(2,1)} %x_hbm.1, f32[2,1024]{1,0:T(2,128)} %lna_hbm.1, f32[2,1024]{1,0:T(2,128)} %lnm_hbm.1, bf16[2304,1024]{1,0:T(8,128)(2,1)} %bitcast.10, ...), custom_call_target="tpu_custom_call" | custom-call | tf_op jit(solution)/shard_map/layer/pallas_call | solution.py:454
  55.3 0.7 %finish.1 = (bf16[128,1024]{1,0:T(8,128)(2,1)}, bf16[16,2,64]{2,1,0:T(2,128)(2,1)}, bf16[16,2,64]{2,1,0:T(2,128)(2,1)}) custom-call(bf16[128,1024]{1,0:T(8,128)(2,1)S(1)} %get-tuple-element.6.x_ref, bf16[16,128]{1,0:T(8,128)(2,1)S(1)} %get-tuple-element.7.k_ref, bf16[16,128]{1,0:T(8,128)(2,1)S(1)} %get-tuple-element.8.v_ref), custom_call_target="tpu_custom_call" | custom-call | tf_op jit(solution)/shard_map/finish/pallas_call | solution.py:505

commit v5 on v3

--- a/solution.py
+++ b/solution.py
@@ -14,29 +14,23 @@
 F32 = jnp.float32
 BF16 = jnp.bfloat16
 VMEM_LIMIT = 58 << 20
-GROUPS_OF_ROWS = 2
+GROUPS_OF_ROWS = 1
 NN = (((1,), (0,)), ((), ()))
 NT = (((1,), (1,)), ((), ()))
 PIECES = ((2, 0), (2, 1), (1, 1), (3, 0), (1, 0), (3, 1), (0, 0), (0, 1))
 ARRIVALS = ((0, 0), (0, 1), (3, 0), (1, 1), (3, 1), (1, 0), (2, 0), (2, 1))
 
 ORDER = (
-    ("qmm", 1), ("qmm", 0), ("umm", 0, 1), ("umm", 0, 2), ("qm", "2r"), ("qm", "1l"),
-    ("umm", 0, 0), ("umm", 0, 5), ("um", 0, "1l"), ("qm", "1r"), ("umm", 1, 1), ("um", 0, "2r"),
-    ("umm", 1, 3), ("um", 0, "1r"), ("umm", 1, 4), ("umm", 1, 5), ("umm", 0, 4), ("um", 1, "2l"),
-    ("umm", 1, 0), ("um", 1, "1l"), ("umm", 0, 6), ("umm", 0, 7), ("umm", 1, 6), ("qm", "3l"),
-    ("um", 1, "1r"), ("qm", "2l"), ("umm", 1, 2), ("umm", 0, 3), ("qm", "3r"), ("umm", 1, 7),
-    ("um", 0, "3l"), ("um", 1, "2r"), ("um", 0, "2l"), ("um", 0, "3r"), ("um", 1, "3l"), ("um", 1, "3r"),
-    ("qt", 1), ("att", 1), ("c", "1l"), ("qt", 0), ("c", "2r"), ("att", 0),
-    ("c", "2l"), ("c", "1r"), ("a", 0, "1"), ("a", 0, "2r"), ("dmm", 0, 1), ("a", 0, "0"),
-    ("a", 0, "2l"), ("a", 1, "0"), ("a", 1, "1"), ("a", 1, "2r"), ("a", 1, "2l"), ("dmm", 0, 0),
-    ("pc", "2r"), ("c", "3l"), ("dmm", 1, 0), ("c", "3r"), ("dmm", 1, 1), ("pc", "2l"),
-    ("ap", 0, "2r"), ("a", 0, "3l"), ("dmm", 0, 4), ("a", 0, "3r"), ("dmm", 0, 3), ("ap", 0, "2l"),
-    ("dmm", 0, 2), ("a", 1, "3r"), ("dmm", 0, 5), ("a", 1, "3l"), ("dmm", 1, 2), ("ap", 1, "2r"),
-    ("dmm", 1, 3), ("ap", 1, "2l"), ("pc", "3r"), ("dmm", 1, 4), ("dmm", 1, 5), ("pc", "3l"),
-    ("ap", 0, "3r"), ("ap", 0, "3l"), ("amm",), ("dmm", 0, 6), ("ap", 1, "3r"), ("dmm", 0, 7),
-    ("ysc", 0), ("ap", 1, "3l"), ("dmm", 1, 6), ("dmm", 1, 7), ("ysc", 1), ("yga", 0),
-    ("yga", 1),
+    ("qmm", 1), ("qmm", 0), ("umm", 0, 0), ("qm", "2r"), ("qm", "1l"), ("umm", 0, 1),
+    ("umm", 0, 2), ("qm", "1r"), ("um", 0, "1r"), ("qm", "2l"), ("umm", 0, 7), ("um", 0, "1l"),
+    ("umm", 0, 5), ("um", 0, "2r"), ("umm", 0, 4), ("umm", 0, 6), ("qm", "3l"), ("umm", 0, 3),
+    ("qm", "3r"), ("um", 0, "2l"), ("um", 0, "3r"), ("um", 0, "3l"), ("qt", 1), ("att", 1),
+    ("c", "1l"), ("c", "2r"), ("qt", 0), ("att", 0), ("c", "1r"), ("c", "2l"),
+    ("a", 0, "0"), ("a", 0, "1"), ("a", 0, "2r"), ("a", 0, "2l"), ("pc", "2r"), ("c", "3l"),
+    ("c", "3r"), ("dmm", 0, 1), ("pc", "2l"), ("dmm", 0, 0), ("a", 0, "3r"), ("a", 0, "3l"),
+    ("dmm", 0, 2), ("dmm", 0, 3), ("ap", 0, "2r"), ("ap", 0, "2l"), ("pc", "3r"), ("pc", "3l"),
+    ("dmm", 0, 4), ("dmm", 0, 5), ("amm",), ("ap", 0, "3r"), ("ap", 0, "3l"), ("dmm", 0, 6),
+    ("dmm", 0, 7), ("ysc", 0), ("yga", 0),
 )
 
 

time: 56 us -> 54.7 us (0.977)
  Pallas kernels: 55.3 us -> 53.9 us
    pallas_call x1, Pallas kernels: 54.6 us -> 53.2 us  [local_layer(): pl.pallas_call(functools.partial(layer_kernel, W, NY), name='layer', out_...]
where the time goes in v5:
time: 54.7 us; the launch traced here: 54.6 us
  Pallas kernels  53.9 us (99%)
  between operations  0.64 us (1%)
    pallas_call x1, Pallas kernels, local_layer(): pl.pallas_call(functools.partial(layer_kernel, W, NY), name='layer', out_...  53.2 us

profile of v5, /device:TPU:97, one launch (start us, length us, event | category | flops | bytes accessed | tf_op | source)
XLA Modules:
  0.0 54.6 jit_solution(5686809819606163316)
XLA Ops:
  0.6 53.2 %layer.1 = (bf16[128,1024]{1,0:T(8,128)(2,1)S(1)}, bf16[16,128]{1,0:T(8,128)(2,1)S(1)}, bf16[16,128]{1,0:T(8,128)(2,1)S(1)}) custom-call(s32[16]{0:T(128)} %pos_hbm.1, bf16[128,1024]{1,0:T(8,128)(2,1)} %x_hbm.1, f32[2,1024]{1,0:T(2,128)} %lna_hbm.1, f32[2,1024]{1,0:T(2,128)} %lnm_hbm.1, bf16[2304,1024]{1,0:T(8,128)(2,1)} %bitcast.10, ...), custom_call_target="tpu_custom_call" | custom-call | tf_op jit(solution)/shard_map/layer/pallas_call | solution.py:418
  53.8 0.7 %finish.1 = (bf16[128,1024]{1,0:T(8,128)(2,1)}, bf16[16,2,64]{2,1,0:T(2,128)(2,1)}, bf16[16,2,64]{2,1,0:T(2,128)(2,1)}) custom-call(bf16[128,1024]{1,0:T(8,128)(2,1)S(1)} %get-tuple-element.6.x_ref, bf16[16,128]{1,0:T(8,128)(2,1)S(1)} %get-tuple-element.7.k_ref, bf16[16,128]{1,0:T(8,128)(2,1)S(1)} %get-tuple-element.8.v_ref), custom_call_target="tpu_custom_call" | custom-call | tf_op jit(solution)/shard_map/finish/pallas_call | solution.py:469

commit v6 on v5

--- a/solution.py
+++ b/solution.py
@@ -14,23 +14,27 @@
 F32 = jnp.float32
 BF16 = jnp.bfloat16
 VMEM_LIMIT = 58 << 20
-GROUPS_OF_ROWS = 1
+GROUPS_OF_ROWS = 2
+GROUPS_OF_COLUMNS = 2
 NN = (((1,), (0,)), ((), ()))
 NT = (((1,), (1,)), ((), ()))
 PIECES = ((2, 0), (2, 1), (1, 1), (3, 0), (1, 0), (3, 1), (0, 0), (0, 1))
 ARRIVALS = ((0, 0), (0, 1), (3, 0), (1, 1), (3, 1), (1, 0), (2, 0), (2, 1))
 
 ORDER = (
-    ("qmm", 1), ("qmm", 0), ("umm", 0, 0), ("qm", "2r"), ("qm", "1l"), ("umm", 0, 1),
-    ("umm", 0, 2), ("qm", "1r"), ("um", 0, "1r"), ("qm", "2l"), ("umm", 0, 7), ("um", 0, "1l"),
-    ("umm", 0, 5), ("um", 0, "2r"), ("umm", 0, 4), ("umm", 0, 6), ("qm", "3l"), ("umm", 0, 3),
-    ("qm", "3r"), ("um", 0, "2l"), ("um", 0, "3r"), ("um", 0, "3l"), ("qt", 1), ("att", 1),
-    ("c", "1l"), ("c", "2r"), ("qt", 0), ("att", 0), ("c", "1r"), ("c", "2l"),
-    ("a", 0, "0"), ("a", 0, "1"), ("a", 0, "2r"), ("a", 0, "2l"), ("pc", "2r"), ("c", "3l"),
-    ("c", "3r"), ("dmm", 0, 1), ("pc", "2l"), ("dmm", 0, 0), ("a", 0, "3r"), ("a", 0, "3l"),
-    ("dmm", 0, 2), ("dmm", 0, 3), ("ap", 0, "2r"), ("ap", 0, "2l"), ("pc", "3r"), ("pc", "3l"),
-    ("dmm", 0, 4), ("dmm", 0, 5), ("amm",), ("ap", 0, "3r"), ("ap", 0, "3l"), ("dmm", 0, 6),
-    ("dmm", 0, 7), ("ysc", 0), ("yga", 0),
+    ("qmm", 0), ("qmm", 1), ("umm", 1), ("qm", "1r"), ("qm", "2l"), ("umm", 0),
+    ("umm", 6), ("qm", "1l"), ("qm", "2r"), ("um", 1, "1l"), ("um", 0, "1l"), ("umm", 4),
+    ("um", 1, "1r"), ("umm", 7), ("um", 0, "1r"), ("umm", 3), ("umm", 2), ("qm", "3r"),
+    ("umm", 5), ("um", 0, "2l"), ("qm", "3l"), ("um", 1, "2l"), ("um", 1, "2r"), ("um", 0, "2r"),
+    ("um", 1, "3l"), ("um", 1, "3r"), ("um", 0, "3l"), ("um", 0, "3r"), ("qt", 0), ("att", 0),
+    ("c", "2l"), ("qt", 1), ("att", 1), ("c", "1r"), ("c", "2r"), ("c", "1l"),
+    ("a", 1, "0"), ("a", 1, "2l"), ("a", 1, "1"), ("a", 1, "2r"), ("a", 0, "1"), ("a", 0, "0"),
+    ("a", 0, "2l"), ("a", 0, "2r"), ("pc", "2l"), ("c", "3r"), ("dmm", 1), ("c", "3l"),
+    ("pc", "2r"), ("dmm", 0), ("a", 1, "3r"), ("ap", 1, "2l"), ("ap", 1, "2r"), ("a", 1, "3l"),
+    ("a", 0, "3l"), ("a", 0, "3r"), ("dmm", 3), ("ap", 0, "2r"), ("ap", 0, "2l"), ("dmm", 2),
+    ("pc", "3l"), ("pc", "3r"), ("dmm", 4), ("dmm", 5), ("ap", 1, "3l"), ("ap", 1, "3r"),
+    ("amm",), ("ap", 0, "3l"), ("ap", 0, "3r"), ("dmm", 7, 1), ("dmm", 6, 1), ("ysc", 1),
+    ("dmm", 6, 0), ("dmm", 7, 0), ("ysc", 0), ("yga", 1), ("yga", 0),
 )
 
 
@@ -52,7 +56,9 @@
     R, D = x_v.shape
     NG = GROUPS_OF_ROWS
     RG = R // NG
-    RY = RG // NY
+    RY = R // NY
+    NC = GROUPS_OF_COLUMNS
+    DC = D // NC
     RB = R // W
     G, HD = kvrot.shape[0], k_v.shape[1]
     L = k_v.shape[2]
@@ -200,18 +206,18 @@
     def qm(key):
         leg("q", key, qkv_own, qsend, qrecv)
 
-    def umm(r, i):
+    def umm(i):
         need(("up", i))
-        hm = hm_v[r * RG:(r + 1) * RG, :]
         for k in range(2):
-            upart[r, i, k] = dot(hm, wup_v[i, :, k * HB:(k + 1) * HB]).astype(BF16)
-        send(("us", r, i), upart.at[r, i, 1 - c], usib.at[r, i], "tpw", sib)
+            upart[i, k] = dot(hm_v[...], wup_v[i, :, k * HB:(k + 1) * HB]).astype(BF16)
+        send(("us", i), upart.at[i, 1 - c], usib.at[i], "tpw", sib)
 
     def up_own(r):
         def own(o, h):
             i = PIECES.index((o, h))
-            arrived(("us", r, i))
-            return upart[r, i, c].astype(F32) + usib[r, i].astype(F32)
+            arrived(("us", i))
+            rows = slice(r * RG, (r + 1) * RG)
+            return upart[i, c, rows].astype(F32) + usib[i, rows].astype(F32)
 
         return own
 
@@ -221,8 +227,8 @@
     mine = pl.ds(pl.multiple_of(c * HB, HB), HB)
 
     def act_send(r, name, o, h, to, to_o):
-        src = act_all.at[r, ARRIVALS.index((o, h)), :, mine]
-        dst = act_all.at[r, ARRIVALS.index((to_o, h)), :, mine]
+        src = act_all.at[ARRIVALS.index((o, h)), pl.ds(r * RG, RG), mine]
+        dst = act_all.at[ARRIVALS.index((to_o, h)), pl.ds(r * RG, RG), mine]
         send(("a", r, name), src, dst, "tpw", to)
 
     def act(r, key):
@@ -230,7 +236,7 @@
             h = int(key)
             pre = total(("u", r), h, up_own(r), urecv.at[r])
             val = 0.5 * pre * (1.0 + lax.erf(pre * (2.0 ** -0.5)))
-            act_all[r, ARRIVALS.index((0, h)), :, mine] = val.astype(BF16)
+            act_all[ARRIVALS.index((0, h)), r * RG:(r + 1) * RG, mine] = val.astype(BF16)
             if h == 0:
                 act_send(r, "1r", 0, 0, right, 3)
             else:
@@ -256,18 +262,23 @@
 
     begun = set()
 
-    def accumulate(r, part):
-        if r in begun:
-            acc[r] += part
+    def accumulate(part, *j):
+        cols = slice(j[0] * DC, (j[0] + 1) * DC) if j else slice(0, D)
+        if begun:
+            acc[:, cols] += part
         else:
-            acc[r] = part
-            begun.add(r)
-
-    def dmm(r, i):
+            acc[...] = part
+            begun.add(0)
+
+    def dmm(i, *j):
         o, h = ARRIVALS[i]
-        arrived(("a", r, ("s", o, h)))
+        for r in range(NG):
+            arrived(("a", r, ("s", o, h)))
         need(("down", i))
-        accumulate(r, dot(act_all[r, i], wdn_v[i]))
+        if j:
+            accumulate(dot(act_all[i], wdn_v[i, :, j[0] * DC:(j[0] + 1) * DC]), *j)
+        else:
+            accumulate(dot(act_all[i], wdn_v[i]))
 
     scale = HD ** -0.5
     when = lax.broadcasted_iota(jnp.int32, (2 * QT, L), 1)
@@ -348,27 +359,26 @@
         need("out")
         n = QT * 128
         for g in range(G):
-            part = dot(ctx_all[:, g].reshape(R, n), wout_v[g * n:(g + 1) * n, :])
-            for r in range(NG):
-                accumulate(r, part[r * RG:(r + 1) * RG])
-
-    def ysc(r):
-        ysend[r] = acc[r].astype(BF16)
+            accumulate(dot(ctx_all[:, g].reshape(R, n), wout_v[g * n:(g + 1) * n, :]))
+
+    def ysc(j):
+        ysend[j] = acc[:, j * DC:(j + 1) * DC].astype(BF16)
         for i in (2, 1, 3):
             to = lax.rem(y + i, NY)
             rows = pl.ds(pl.multiple_of(to * RY, RY), RY)
-            send(("y", r, i), ysend.at[r, rows], yrecv.at[r, i - 1], "tph", to)
-
-    def yga(r):
-        start = pl.multiple_of(y * RY, RY)
-        tot = acc[r, pl.ds(start, RY), :]
+            send(("y", j, i), ysend.at[j, rows], yrecv.at[j, i - 1], "tph", to)
+
+    def yga(j):
+        rows = pl.ds(pl.multiple_of(y * RY, RY), RY)
+        cols = slice(j * DC, (j + 1) * DC)
+        tot = acc[rows, cols]
         for i in range(1, NY):
-            arrived(("y", r, i))
-            tot = tot + yrecv[r, i - 1].astype(F32)
-        rows = pl.ds(pl.multiple_of(r * RG + start, RY), RY)
-        xout_ref[rows, :] = (x_v[rows, :].astype(F32) + tot).astype(BF16)
+            arrived(("y", j, i))
+            tot = tot + yrecv[j, i - 1].astype(F32)
+        xout_ref[rows, cols] = (x_v[rows, cols].astype(F32) + tot).astype(BF16)
+        block = xout_ref.at[rows, pl.ds(j * DC, DC)]
         for i in (2, 1, 3):
-            send(("z", r, i), xout_ref.at[rows, :], xout_ref.at[rows, :], "tph", lax.rem(y + i, NY))
+            send(("z", j, i), block, block, "tph", lax.rem(y + i, NY))
 
     steps = {
         "qmm": qmm, "qm": qm, "umm": umm, "um": um, "a": act, "ap": ap, "dmm": dmm, "qt": qt, "att": att,
@@ -412,7 +422,8 @@
         wqkv_t = jnp.transpose(w_qkv, (1, 2, 3, 0)).reshape(G * qw, D)
         k_t = jnp.swapaxes(k_cache, 2, 3).reshape(RB * G, HD, L)
         v_t = jnp.swapaxes(v_cache, 2, 3).reshape(RB * G, HD, L)
-        n_messages = 7 + 2 + 6 + NG * 8 + NG * 6 + NG * 14 + 14 + NG * 6
+        NC = GROUPS_OF_COLUMNS
+        n_messages = W - 1 + 2 + 6 + 8 + NG * 6 + NG * 14 + 14 + NC * 6
         any_spec = pl.BlockSpec(memory_space=pl.ANY)
         vmem_spec = pl.BlockSpec(memory_space=pltpu.VMEM)
         x_out, k_new, v_new = pl.pallas_call(
@@ -448,14 +459,14 @@
                 pltpu.VMEM((G, RB, 128), F32),
                 pltpu.VMEM((G, QT * RB, 128), F32),
                 pltpu.VMEM((W, G, RB, cw), BF16),
-                pltpu.VMEM((NG, 8, 2, RG, HB), BF16),
-                pltpu.VMEM((NG, 8, RG, HB), BF16),
+                pltpu.VMEM((8, 2, R, HB), BF16),
+                pltpu.VMEM((8, R, HB), BF16),
                 pltpu.VMEM((NG, 6, RG, HB), BF16),
                 pltpu.VMEM((NG, 6, RG, HB), BF16),
-                pltpu.VMEM((NG, 8, RG, 2 * HB), BF16),
-                pltpu.VMEM((NG, RG, D), F32),
-                pltpu.VMEM((NG, RG, D), BF16),
-                pltpu.VMEM((NG, NY - 1, RG // NY, D), BF16),
+                pltpu.VMEM((8, R, 2 * HB), BF16),
+                pltpu.VMEM((R, D), F32),
+                pltpu.VMEM((NC, R, D // NC), BF16),
+                pltpu.VMEM((NC, NY - 1, R // NY, D // NC), BF16),
                 pltpu.SemaphoreType.DMA((32,)),
                 pltpu.SemaphoreType.DMA((n_messages,)),
                 pltpu.SemaphoreType.DMA((n_messages,)),

time: 54.7 us -> 53.6 us (0.980)
  Pallas kernels: 53.9 us -> 52.9 us
    pallas_call x1, Pallas kernels: 53.2 us -> 52.1 us  [local_layer(): pl.pallas_call(functools.partial(layer_kernel, W, NY), name='layer', out_...]
where the time goes in v6:
time: 53.6 us; the launch traced here: 53.5 us
  Pallas kernels  52.9 us (99%)
  between operations  0.64 us (1%)
    pallas_call x1, Pallas kernels, local_layer(): pl.pallas_call(functools.partial(layer_kernel, W, NY), name='layer', out_...  52.1 us

profile of v6, /device:TPU:97, one launch (start us, length us, event | category | flops | bytes accessed | tf_op | source)
XLA Modules:
  0.0 53.5 jit_solution(6093935703032783375)
XLA Ops:
  0.6 52.1 %layer.1 = (bf16[128,1024]{1,0:T(8,128)(2,1)S(1)}, bf16[16,128]{1,0:T(8,128)(2,1)S(1)}, bf16[16,128]{1,0:T(8,128)(2,1)S(1)}) custom-call(s32[16]{0:T(128)} %pos_hbm.1, bf16[128,1024]{1,0:T(8,128)(2,1)} %x_hbm.1, f32[2,1024]{1,0:T(2,128)} %lna_hbm.1, f32[2,1024]{1,0:T(2,128)} %lnm_hbm.1, bf16[2304,1024]{1,0:T(8,128)(2,1)} %bitcast.10, ...), custom_call_target="tpu_custom_call" | custom-call | tf_op jit(solution)/shard_map/layer/pallas_call | solution.py:429
  52.8 0.7 %finish.1 = (bf16[128,1024]{1,0:T(8,128)(2,1)}, bf16[16,2,64]{2,1,0:T(2,128)(2,1)}, bf16[16,2,64]{2,1,0:T(2,128)(2,1)}) custom-call(bf16[128,1024]{1,0:T(8,128)(2,1)S(1)} %get-tuple-element.6.x_ref, bf16[16,128]{1,0:T(8,128)(2,1)S(1)} %get-tuple-element.7.k_ref, bf16[16,128]{1,0:T(8,128)(2,1)S(1)} %get-tuple-element.8.v_ref), custom_call_target="tpu_custom_call" | custom-call | tf_op jit(solution)/shard_map/finish/pallas_call | solution.py:480

commit v7 on v6

--- a/solution.py
+++ b/solution.py
@@ -14,27 +14,25 @@
 F32 = jnp.float32
 BF16 = jnp.bfloat16
 VMEM_LIMIT = 58 << 20
-GROUPS_OF_ROWS = 2
-GROUPS_OF_COLUMNS = 2
+GROUPS_OF_ROWS = 1
+LAST_GROUPS = 2
 NN = (((1,), (0,)), ((), ()))
 NT = (((1,), (1,)), ((), ()))
 PIECES = ((2, 0), (2, 1), (1, 1), (3, 0), (1, 0), (3, 1), (0, 0), (0, 1))
 ARRIVALS = ((0, 0), (0, 1), (3, 0), (1, 1), (3, 1), (1, 0), (2, 0), (2, 1))
 
 ORDER = (
-    ("qmm", 0), ("qmm", 1), ("umm", 1), ("qm", "1r"), ("qm", "2l"), ("umm", 0),
-    ("umm", 6), ("qm", "1l"), ("qm", "2r"), ("um", 1, "1l"), ("um", 0, "1l"), ("umm", 4),
-    ("um", 1, "1r"), ("umm", 7), ("um", 0, "1r"), ("umm", 3), ("umm", 2), ("qm", "3r"),
-    ("umm", 5), ("um", 0, "2l"), ("qm", "3l"), ("um", 1, "2l"), ("um", 1, "2r"), ("um", 0, "2r"),
-    ("um", 1, "3l"), ("um", 1, "3r"), ("um", 0, "3l"), ("um", 0, "3r"), ("qt", 0), ("att", 0),
-    ("c", "2l"), ("qt", 1), ("att", 1), ("c", "1r"), ("c", "2r"), ("c", "1l"),
-    ("a", 1, "0"), ("a", 1, "2l"), ("a", 1, "1"), ("a", 1, "2r"), ("a", 0, "1"), ("a", 0, "0"),
-    ("a", 0, "2l"), ("a", 0, "2r"), ("pc", "2l"), ("c", "3r"), ("dmm", 1), ("c", "3l"),
-    ("pc", "2r"), ("dmm", 0), ("a", 1, "3r"), ("ap", 1, "2l"), ("ap", 1, "2r"), ("a", 1, "3l"),
-    ("a", 0, "3l"), ("a", 0, "3r"), ("dmm", 3), ("ap", 0, "2r"), ("ap", 0, "2l"), ("dmm", 2),
-    ("pc", "3l"), ("pc", "3r"), ("dmm", 4), ("dmm", 5), ("ap", 1, "3l"), ("ap", 1, "3r"),
-    ("amm",), ("ap", 0, "3l"), ("ap", 0, "3r"), ("dmm", 7, 1), ("dmm", 6, 1), ("ysc", 1),
-    ("dmm", 6, 0), ("dmm", 7, 0), ("ysc", 0), ("yga", 1), ("yga", 0),
+    ("qmm", 0), ("qmm", 1), ("umm", 1), ("umm", 0), ("qm", "2l"), ("qm", "1r"),
+    ("umm", 5), ("qm", "2r"), ("qm", "1l"), ("umm", 6), ("um", 0, "1l"), ("umm", 7),
+    ("um", 0, "1r"), ("umm", 2), ("umm", 3), ("umm", 4), ("qm", "3r"), ("um", 0, "2r"),
+    ("um", 0, "2l"), ("qm", "3l"), ("um", 0, "3l"), ("um", 0, "3r"), ("qt", 0), ("att", 0),
+    ("c", "1r"), ("c", "2l"), ("qt", 1), ("att", 1), ("c", "1l"), ("c", "2r"),
+    ("a", 0, "1"), ("a", 0, "0"), ("a", 0, "2r"), ("a", 0, "2l"), ("pc", "2l"), ("c", "3r"),
+    ("dmm", 1), ("pc", "2r"), ("c", "3l"), ("dmm", 0), ("a", 0, "3r"), ("a", 0, "3l"),
+    ("dmm", 2), ("dmm", 3), ("ap", 0, "2l"), ("ap", 0, "2r"), ("pc", "3l"), ("pc", "3r"),
+    ("dmm", 5), ("dmm", 4), ("at", "3l", 0), ("at", "3r", 0), ("amm",), ("at", "3l", 1),
+    ("dmm", 6, 0), ("at", "3r", 1), ("dmm", 7, 0), ("ysc", 0), ("dmm", 7, 1), ("dmm", 6, 1),
+    ("ysc", 1), ("yga", 0), ("yga", 1),
 )
 
 
@@ -56,9 +54,8 @@
     R, D = x_v.shape
     NG = GROUPS_OF_ROWS
     RG = R // NG
-    RY = R // NY
-    NC = GROUPS_OF_COLUMNS
-    DC = D // NC
+    RL = R // LAST_GROUPS
+    RY = RL // NY
     RB = R // W
     G, HD = kvrot.shape[0], k_v.shape[1]
     L = k_v.shape[2]
@@ -226,9 +223,10 @@
 
     mine = pl.ds(pl.multiple_of(c * HB, HB), HB)
 
-    def act_send(r, name, o, h, to, to_o):
-        src = act_all.at[ARRIVALS.index((o, h)), pl.ds(r * RG, RG), mine]
-        dst = act_all.at[ARRIVALS.index((to_o, h)), pl.ds(r * RG, RG), mine]
+    def act_send(r, name, o, h, to, to_o, *part):
+        rows = pl.ds(part[0] * RL, RL) if part else pl.ds(r * RG, RG)
+        src = act_all.at[ARRIVALS.index((o, h)), rows, mine]
+        dst = act_all.at[ARRIVALS.index((to_o, h)), rows, mine]
         send(("a", r, name), src, dst, "tpw", to)
 
     def act(r, key):
@@ -248,35 +246,41 @@
             act_send(r, "2l", 0, 0, left, 1)
         elif key == "3r":
             arrived(("a", r, "1r"))
-            act_send(r, "3r", 3, 0, right, 2)
+            for j in range(LAST_GROUPS):
+                act_send(r, ("3r", j), 3, 0, right, 2, j)
             act_send(r, ("s", 3, 0), 3, 0, sib, 3)
         else:
             arrived(("a", r, "1l"))
-            act_send(r, "3l", 1, 1, left, 2)
+            for j in range(LAST_GROUPS):
+                act_send(r, ("3l", j), 1, 1, left, 2, j)
             act_send(r, ("s", 1, 1), 1, 1, sib, 1)
 
     def ap(r, key):
-        o, h = {"2r": (3, 1), "2l": (1, 0), "3r": (2, 0), "3l": (2, 1)}[key]
+        o, h = {"2r": (3, 1), "2l": (1, 0)}[key]
         arrived(("a", r, key))
         act_send(r, ("s", o, h), o, h, sib, o)
 
+    def at(key, j):
+        h = {"3r": 0, "3l": 1}[key]
+        arrived(("a", 0, (key, j)))
+        act_send(0, ("s", 2, h, j), 2, h, sib, 2, j)
+
     begun = set()
 
     def accumulate(part, *j):
-        cols = slice(j[0] * DC, (j[0] + 1) * DC) if j else slice(0, D)
+        rows = slice(j[0] * RL, (j[0] + 1) * RL) if j else slice(0, R)
         if begun:
-            acc[:, cols] += part
+            acc[rows, :] += part
         else:
             acc[...] = part
             begun.add(0)
 
     def dmm(i, *j):
         o, h = ARRIVALS[i]
-        for r in range(NG):
-            arrived(("a", r, ("s", o, h)))
+        arrived(("a", 0, ("s", o, h) + j))
         need(("down", i))
         if j:
-            accumulate(dot(act_all[i], wdn_v[i, :, j[0] * DC:(j[0] + 1) * DC]), *j)
+            accumulate(dot(act_all[i, j[0] * RL:(j[0] + 1) * RL, :], wdn_v[i]), *j)
         else:
             accumulate(dot(act_all[i], wdn_v[i]))
 
@@ -362,26 +366,24 @@
             accumulate(dot(ctx_all[:, g].reshape(R, n), wout_v[g * n:(g + 1) * n, :]))
 
     def ysc(j):
-        ysend[j] = acc[:, j * DC:(j + 1) * DC].astype(BF16)
+        ysend[j] = acc[j * RL:(j + 1) * RL, :].astype(BF16)
         for i in (2, 1, 3):
             to = lax.rem(y + i, NY)
             rows = pl.ds(pl.multiple_of(to * RY, RY), RY)
             send(("y", j, i), ysend.at[j, rows], yrecv.at[j, i - 1], "tph", to)
 
     def yga(j):
-        rows = pl.ds(pl.multiple_of(y * RY, RY), RY)
-        cols = slice(j * DC, (j + 1) * DC)
-        tot = acc[rows, cols]
+        rows = pl.ds(pl.multiple_of(j * RL + y * RY, RY), RY)
+        tot = acc[rows, :]
         for i in range(1, NY):
             arrived(("y", j, i))
             tot = tot + yrecv[j, i - 1].astype(F32)
-        xout_ref[rows, cols] = (x_v[rows, cols].astype(F32) + tot).astype(BF16)
-        block = xout_ref.at[rows, pl.ds(j * DC, DC)]
+        xout_ref[rows, :] = (x_v[rows, :].astype(F32) + tot).astype(BF16)
         for i in (2, 1, 3):
-            send(("z", j, i), block, block, "tph", lax.rem(y + i, NY))
+            send(("z", j, i), xout_ref.at[rows, :], xout_ref.at[rows, :], "tph", lax.rem(y + i, NY))
 
     steps = {
-        "qmm": qmm, "qm": qm, "umm": umm, "um": um, "a": act, "ap": ap, "dmm": dmm, "qt": qt, "att": att,
+        "qmm": qmm, "qm": qm, "umm": umm, "um": um, "a": act, "ap": ap, "at": at, "dmm": dmm, "qt": qt, "att": att,
         "c": ctx, "pc": pc, "amm": amm, "ysc": ysc, "yga": yga,
     }
     for step in ORDER:
@@ -422,8 +424,8 @@
         wqkv_t = jnp.transpose(w_qkv, (1, 2, 3, 0)).reshape(G * qw, D)
         k_t = jnp.swapaxes(k_cache, 2, 3).reshape(RB * G, HD, L)
         v_t = jnp.swapaxes(v_cache, 2, 3).reshape(RB * G, HD, L)
-        NC = GROUPS_OF_COLUMNS
-        n_messages = W - 1 + 2 + 6 + 8 + NG * 6 + NG * 14 + 14 + NC * 6
+        NL = LAST_GROUPS
+        n_messages = W - 1 + 2 + 6 + 8 + NG * 6 + NG * 10 + 4 * NL + 14 + NL * 6
         any_spec = pl.BlockSpec(memory_space=pl.ANY)
         vmem_spec = pl.BlockSpec(memory_space=pltpu.VMEM)
         x_out, k_new, v_new = pl.pallas_call(
@@ -465,8 +467,8 @@
                 pltpu.VMEM((NG, 6, RG, HB), BF16),
                 pltpu.VMEM((8, R, 2 * HB), BF16),
                 pltpu.VMEM((R, D), F32),
-                pltpu.VMEM((NC, R, D // NC), BF16),
-                pltpu.VMEM((NC, NY - 1, R // NY, D // NC), BF16),
+                pltpu.VMEM((NL, R // NL, D), BF16),
+                pltpu.VMEM((NL, NY - 1, R // NL // NY, D), BF16),
                 pltpu.SemaphoreType.DMA((32,)),
                 pltpu.SemaphoreType.DMA((n_messages,)),
                 pltpu.SemaphoreType.DMA((n_messages,)),

time: 53.6 us -> 53.9 us (level)
  no operation moved by 1% of the time
where the time goes in v7:
time: 53.9 us; the launch traced here: 53.8 us
  Pallas kernels  53.2 us (99%)
  between operations  0.64 us (1%)
    pallas_call x1, Pallas kernels, local_layer(): pl.pallas_call(functools.partial(layer_kernel, W, NY), name='layer', out_...  52.4 us

profile of v7, /device:TPU:97, one launch (start us, length us, event | category | flops | bytes accessed | tf_op | source)
XLA Modules:
  0.0 53.8 jit_solution(11440106509373510406)
XLA Ops:
  0.6 52.4 %layer.1 = (bf16[128,1024]{1,0:T(8,128)(2,1)S(1)}, bf16[16,128]{1,0:T(8,128)(2,1)S(1)}, bf16[16,128]{1,0:T(8,128)(2,1)S(1)}) custom-call(s32[16]{0:T(128)} %pos_hbm.1, bf16[128,1024]{1,0:T(8,128)(2,1)} %x_hbm.1, f32[2,1024]{1,0:T(2,128)} %lna_hbm.1, f32[2,1024]{1,0:T(2,128)} %lnm_hbm.1, bf16[2304,1024]{1,0:T(8,128)(2,1)} %bitcast.10, ...), custom_call_target="tpu_custom_call" | custom-call | tf_op jit(solution)/shard_map/layer/pallas_call | solution.py:431
  53.1 0.7 %finish.1 = (bf16[128,1024]{1,0:T(8,128)(2,1)}, bf16[16,2,64]{2,1,0:T(2,128)(2,1)}, bf16[16,2,64]{2,1,0:T(2,128)(2,1)}) custom-call(bf16[128,1024]{1,0:T(8,128)(2,1)S(1)} %get-tuple-element.6.x_ref, bf16[16,128]{1,0:T(8,128)(2,1)S(1)} %get-tuple-element.7.k_ref, bf16[16,128]{1,0:T(8,128)(2,1)S(1)} %get-tuple-element.8.v_ref), custom_call_target="tpu_custom_call" | custom-call | tf_op jit(solution)/shard_map/finish/pallas_call | solution.py:482

commit v8 on v6

--- a/solution.py
+++ b/solution.py
@@ -101,13 +101,6 @@
     for i, (o, h) in enumerate(PIECES):
         col = pl.multiple_of((chip(o) * 2 + h) * 2 * HB, 2 * HB)
         load(("up", i), wup_hbm.at[:, pl.ds(col, 2 * HB)], wup_v.at[i])
-    load("k", k_hbm, k_v)
-    load("v", v_hbm, v_v)
-    load("out", wout_hbm, wout_v)
-    for i, (o, h) in enumerate(ARRIVALS):
-        row = pl.multiple_of((chip(o) * 2 + h) * 2 * HB, 2 * HB)
-        load(("down", i), wdn_hbm.at[pl.ds(row, 2 * HB), :], wdn_v.at[i])
-
     sent = []
     messages = {}
 
@@ -170,6 +163,14 @@
     cen = (x_v[...].astype(F32) - mean) * rstd
     ha_v[...] = (cen * lna_v[0:1, :] + lna_v[1:2, :]).astype(BF16)
     hm_v[...] = (cen * lnm_v[0:1, :] + lnm_v[1:2, :]).astype(BF16)
+
+    def load_late():
+        load("k", k_hbm, k_v)
+        load("v", v_hbm, v_v)
+        load("out", wout_hbm, wout_v)
+        for i, (o, h) in enumerate(ARRIVALS):
+            row = pl.multiple_of((chip(o) * 2 + h) * 2 * HB, 2 * HB)
+            load(("down", i), wdn_hbm.at[pl.ds(row, 2 * HB), :], wdn_v.at[i])
 
     legs = {
         "1r": (0, 2, 0, None, right), "1l": (1, 2, 1, None, left),
@@ -362,10 +363,10 @@
             accumulate(dot(ctx_all[:, g].reshape(R, n), wout_v[g * n:(g + 1) * n, :]))
 
     def ysc(j):
-        ysend[j] = acc[:, j * DC:(j + 1) * DC].astype(BF16)
         for i in (2, 1, 3):
             to = lax.rem(y + i, NY)
             rows = pl.ds(pl.multiple_of(to * RY, RY), RY)
+            ysend[j, rows, :] = acc[rows, j * DC:(j + 1) * DC].astype(BF16)
             send(("y", j, i), ysend.at[j, rows], yrecv.at[j, i - 1], "tph", to)
 
     def yga(j):
@@ -384,20 +385,31 @@
         "qmm": qmm, "qm": qm, "umm": umm, "um": um, "a": act, "ap": ap, "dmm": dmm, "qt": qt, "att": att,
         "c": ctx, "pc": pc, "amm": amm, "ysc": ysc, "yga": yga,
     }
-    for step in ORDER:
+    last_up = max(i for i, step in enumerate(ORDER) if step[0] == "umm")
+    first_sum = min(i for i, step in enumerate(ORDER) if step[0] == "yga")
+    done = 0
+    for i, step in enumerate(ORDER):
+        if i == first_sum:
+            for cp in sent:
+                cp.wait_send()
+            done = len(sent)
         steps[step[0]](*step[1:])
+        if i == last_up:
+            load_late()
     for name in messages:
         arrived(name)
-    for cp in sent:
+    for cp in sent[done:]:
         cp.wait_send()
 
 
-def finish_kernel(x_ref, k_ref, v_ref, xout_ref, knew_ref, vnew_ref):
-    xout_ref[...] = x_ref[...]
+def finish_kernel(x_ref, k_ref, v_ref, xout_ref, knew_ref, vnew_ref, sem):
+    cp = pltpu.make_async_copy(x_ref, xout_ref, sem)
+    cp.start()
     hd = knew_ref.shape[2]
     for g in range(knew_ref.shape[1]):
         knew_ref[:, g, :] = k_ref[:, g * hd:(g + 1) * hd]
         vnew_ref[:, g, :] = v_ref[:, g * hd:(g + 1) * hd]
+    cp.wait()
 
 
 def solution(mesh):
@@ -486,7 +498,8 @@
                 jax.ShapeDtypeStruct((RB, G, HD), BF16),
             ),
             in_specs=[vmem_spec] * 3,
-            out_specs=(vmem_spec,) * 3,
+            out_specs=(any_spec, vmem_spec, vmem_spec),
+            scratch_shapes=[pltpu.SemaphoreType.DMA],
         )(*(pltpu.with_memory_space_constraint(a, pltpu.VMEM) for a in (x_out, k_new, v_new)))
 
     cache_spec = P(("dp", "tpw"), "tph", None, None)

time: 53.6 us -> 54.1 us (level)
    pallas_call x1, Pallas kernels: 0.74 us -> 1.32 us  [local_layer(): pl.pallas_call(finish_kernel, name='finish', out_shape=(jax.ShapeDtypeStr...]
where the time goes in v8:
time: 54.1 us; the launch traced here: 54 us
  Pallas kernels  53.3 us (99%)
  between operations  0.64 us (1%)
    pallas_call x1, Pallas kernels, local_layer(): pl.pallas_call(functools.partial(layer_kernel, W, NY), name='layer', out_...  52 us
    pallas_call x1, Pallas kernels, local_layer(): pl.pallas_call(finish_kernel, name='finish', out_shape=(jax.ShapeDtypeStr...  1.32 us

profile of v8, /device:TPU:97, one launch (start us, length us, event | category | flops | bytes accessed | tf_op | source)
XLA Modules:
  0.0 54.0 jit_solution(12454698837049770431)
XLA Ops:
  0.6 52.0 %layer.1 = (bf16[128,1024]{1,0:T(8,128)(2,1)S(1)}, bf16[16,128]{1,0:T(8,128)(2,1)S(1)}, bf16[16,128]{1,0:T(8,128)(2,1)S(1)}) custom-call(s32[16]{0:T(128)} %pos_hbm.1, bf16[128,1024]{1,0:T(8,128)(2,1)} %x_hbm.1, f32[2,1024]{1,0:T(2,128)} %lna_hbm.1, f32[2,1024]{1,0:T(2,128)} %lnm_hbm.1, bf16[2304,1024]{1,0:T(8,128)(2,1)} %bitcast.10, ...), custom_call_target="tpu_custom_call" | custom-call | tf_op jit(solution)/shard_map/layer/pallas_call | solution.py:441
  52.7 1.3 %finish.1 = (bf16[128,1024]{1,0:T(8,128)(2,1)}, bf16[16,2,64]{2,1,0:T(2,128)(2,1)}, bf16[16,2,64]{2,1,0:T(2,128)(2,1)}) custom-call(bf16[128,1024]{1,0:T(8,128)(2,1)S(1)} %get-tuple-element.6.x_ref, bf16[16,128]{1,0:T(8,128)(2,1)S(1)} %get-tuple-element.7.k_ref, bf16[16,128]{1,0:T(8,128)(2,1)S(1)} %get-tuple-element.8.v_ref), custom_call_target="tpu_custom_call" | custom-call | tf_op jit(solution)/shard_map/finish/pallas_call | solution.py:492

commit v9 on v8

--- a/solution.py
+++ b/solution.py
@@ -33,8 +33,8 @@
     ("pc", "2r"), ("dmm", 0), ("a", 1, "3r"), ("ap", 1, "2l"), ("ap", 1, "2r"), ("a", 1, "3l"),
     ("a", 0, "3l"), ("a", 0, "3r"), ("dmm", 3), ("ap", 0, "2r"), ("ap", 0, "2l"), ("dmm", 2),
     ("pc", "3l"), ("pc", "3r"), ("dmm", 4), ("dmm", 5), ("ap", 1, "3l"), ("ap", 1, "3r"),
-    ("amm",), ("ap", 0, "3l"), ("ap", 0, "3r"), ("dmm", 7, 1), ("dmm", 6, 1), ("ysc", 1),
-    ("dmm", 6, 0), ("dmm", 7, 0), ("ysc", 0), ("yga", 1), ("yga", 0),
+    ("amm",), ("ap", 0, "3l"), ("ap", 0, "3r"), ("last", 1), ("ysc", 1), ("last", 0),
+    ("ysc", 0), ("yga", 1), ("yga", 0),
 )
 
 
@@ -271,15 +271,22 @@
             acc[...] = part
             begun.add(0)
 
-    def dmm(i, *j):
+    def ready(i):
         o, h = ARRIVALS[i]
         for r in range(NG):
             arrived(("a", r, ("s", o, h)))
         need(("down", i))
-        if j:
-            accumulate(dot(act_all[i], wdn_v[i, :, j[0] * DC:(j[0] + 1) * DC]), *j)
-        else:
-            accumulate(dot(act_all[i], wdn_v[i]))
+
+    def dmm(i):
+        ready(i)
+        accumulate(dot(act_all[i], wdn_v[i]))
+
+    def last(j):
+        cols = slice(j * DC, (j + 1) * DC)
+        n = len(ARRIVALS)
+        ready(n - 2)
+        ready(n - 1)
+        accumulate(dot(act_all[n - 2], wdn_v[n - 2, :, cols]) + dot(act_all[n - 1], wdn_v[n - 1, :, cols]), j)
 
     scale = HD ** -0.5
     when = lax.broadcasted_iota(jnp.int32, (2 * QT, L), 1)
@@ -382,7 +389,7 @@
             send(("z", j, i), block, block, "tph", lax.rem(y + i, NY))
 
     steps = {
-        "qmm": qmm, "qm": qm, "umm": umm, "um": um, "a": act, "ap": ap, "dmm": dmm, "qt": qt, "att": att,
+        "qmm": qmm, "qm": qm, "umm": umm, "um": um, "a": act, "ap": ap, "dmm": dmm, "last": last, "qt": qt, "att": att,
         "c": ctx, "pc": pc, "amm": amm, "ysc": ysc, "yga": yga,
     }
     last_up = max(i for i, step in enumerate(ORDER) if step[0] == "umm")
@@ -402,14 +409,12 @@
         cp.wait_send()
 
 
-def finish_kernel(x_ref, k_ref, v_ref, xout_ref, knew_ref, vnew_ref, sem):
-    cp = pltpu.make_async_copy(x_ref, xout_ref, sem)
-    cp.start()
+def finish_kernel(x_ref, k_ref, v_ref, xout_ref, knew_ref, vnew_ref):
+    xout_ref[...] = x_ref[...]
     hd = knew_ref.shape[2]
     for g in range(knew_ref.shape[1]):
         knew_ref[:, g, :] = k_ref[:, g * hd:(g + 1) * hd]
         vnew_ref[:, g, :] = v_ref[:, g * hd:(g + 1) * hd]
-    cp.wait()
 
 
 def solution(mesh):
@@ -498,8 +503,7 @@
                 jax.ShapeDtypeStruct((RB, G, HD), BF16),
             ),
             in_specs=[vmem_spec] * 3,
-            out_specs=(any_spec, vmem_spec, vmem_spec),
-            scratch_shapes=[pltpu.SemaphoreType.DMA],
+            out_specs=(vmem_spec,) * 3,
         )(*(pltpu.with_memory_space_constraint(a, pltpu.VMEM) for a in (x_out, k_new, v_new)))
 
     cache_spec = P(("dp", "tpw"), "tph", None, None)

time: 54.1 us -> 53.6 us (level)
    pallas_call x1, Pallas kernels: 1.32 us -> 0.74 us  [local_layer(): pl.pallas_call(finish_kernel, name='finish', out_shape=(jax.ShapeDtypeStr...]
where the time goes in v9:
time: 53.6 us; the launch traced here: 53.5 us
  Pallas kernels  52.9 us (99%)
  between operations  0.64 us (1%)
    pallas_call x1, Pallas kernels, local_layer(): pl.pallas_call(functools.partial(layer_kernel, W, NY), name='layer', out_...  52.1 us

profile of v9, /device:TPU:97, one launch (start us, length us, event | category | flops | bytes accessed | tf_op | source)
XLA Modules:
  0.0 53.5 jit_solution(7532745310482779552)
XLA Ops:
  0.6 52.1 %layer.1 = (bf16[128,1024]{1,0:T(8,128)(2,1)S(1)}, bf16[16,128]{1,0:T(8,128)(2,1)S(1)}, bf16[16,128]{1,0:T(8,128)(2,1)S(1)}) custom-call(s32[16]{0:T(128)} %pos_hbm.1, bf16[128,1024]{1,0:T(8,128)(2,1)} %x_hbm.1, f32[2,1024]{1,0:T(2,128)} %lna_hbm.1, f32[2,1024]{1,0:T(2,128)} %lnm_hbm.1, bf16[2304,1024]{1,0:T(8,128)(2,1)} %bitcast.10, ...), custom_call_target="tpu_custom_call" | custom-call | tf_op jit(solution)/shard_map/layer/pallas_call | solution.py:446
  52.8 0.7 %finish.1 = (bf16[128,1024]{1,0:T(8,128)(2,1)}, bf16[16,2,64]{2,1,0:T(2,128)(2,1)}, bf16[16,2,64]{2,1,0:T(2,128)(2,1)}) custom-call(bf16[128,1024]{1,0:T(8,128)(2,1)S(1)} %get-tuple-element.6.x_ref, bf16[16,128]{1,0:T(8,128)(2,1)S(1)} %get-tuple-element.7.k_ref, bf16[16,128]{1,0:T(8,128)(2,1)S(1)} %get-tuple-element.8.v_ref), custom_call_target="tpu_custom_call" | custom-call | tf_op jit(solution)/shard_map/finish/pallas_call | solution.py:497

commit v10 on v9

--- a/solution.py
+++ b/solution.py
@@ -79,7 +79,8 @@
         return lax.rem(x + o, NX)
 
     barrier = pltpu.get_barrier_semaphore()
-    for i in range(1, W):
+    far_first = sorted(range(1, W), key=lambda i: -min(i, W - i))
+    for i in far_first:
         pl.semaphore_signal(barrier, inc=1, device_id={"tpw": lax.rem(w + i, W)}, device_id_type=MESH)
     for i in range(1, NY):
         pl.semaphore_signal(barrier, inc=1, device_id={"tph": lax.rem(y + i, NY)}, device_id_type=MESH)
@@ -133,7 +134,7 @@
     lane = lax.broadcasted_iota(jnp.int32, (R, 128), 1)
     stat_send[...] = jnp.where(lane == 0, s1, jnp.where(lane == 1, s2, 0.0)).T[0:8, :]
     pl.semaphore_wait(barrier, W - 1 + NY - 1)
-    for i in range(1, W):
+    for i in far_first:
         send(("stat", i), stat_send, stat_recv.at[i - 1], "tpw", lax.rem(w + i, W))
 
     loads["pos"].wait()

time: 53.6 us -> 53.5 us (level)
  no operation moved by 1% of the time
where the time goes in v10:
time: 53.5 us
  Pallas kernels  52.8 us (99%)
  between operations  0.64 us (1%)
    pallas_call x1, Pallas kernels, local_layer(): pl.pallas_call(functools.partial(layer_kernel, W, NY), name='layer', out_...  52.1 us

profile of v10, /device:TPU:97, one launch (start us, length us, event | category | flops | bytes accessed | tf_op | source)
XLA Modules:
  0.0 53.5 jit_solution(11857340253846910609)
XLA Ops:
  0.6 52.1 %layer.1 = (bf16[128,1024]{1,0:T(8,128)(2,1)S(1)}, bf16[16,128]{1,0:T(8,128)(2,1)S(1)}, bf16[16,128]{1,0:T(8,128)(2,1)S(1)}) custom-call(s32[16]{0:T(128)} %pos_hbm.1, bf16[128,1024]{1,0:T(8,128)(2,1)} %x_hbm.1, f32[2,1024]{1,0:T(2,128)} %lna_hbm.1, f32[2,1024]{1,0:T(2,128)} %lnm_hbm.1, bf16[2304,1024]{1,0:T(8,128)(2,1)} %bitcast.10, ...), custom_call_target="tpu_custom_call" | custom-call | tf_op jit(solution)/shard_map/layer/pallas_call | solution.py:447
  52.7 0.7 %finish.1 = (bf16[128,1024]{1,0:T(8,128)(2,1)}, bf16[16,2,64]{2,1,0:T(2,128)(2,1)}, bf16[16,2,64]{2,1,0:T(2,128)(2,1)}) custom-call(bf16[128,1024]{1,0:T(8,128)(2,1)S(1)} %get-tuple-element.6.x_ref, bf16[16,128]{1,0:T(8,128)(2,1)S(1)} %get-tuple-element.7.k_ref, bf16[16,128]{1,0:T(8,128)(2,1)S(1)} %get-tuple-element.8.v_ref), custom_call_target="tpu_custom_call" | custom-call | tf_op jit(solution)/shard_map/finish/pallas_call | solution.py:498
